TPU v7x, 512 devices: a whole 4x8x8 slice. The times are simulated.
512 devices in a mesh: dp: 128 (over z, y, core), tensor: 4 (over x).
Axes of the slice: x: 4, y: 8, z: 8, core: 2. Of those that a mesh axis runs over, the one named last changes fastest.
Arguments:
- hidden: bfloat16 [512, 8, 3584], P('dp', None, 'tensor')
- norm_gain: float32 [3584], replicated, may hold values from 0.5 to 2
- head_weight: bfloat16 [152064, 3584], P(('dp', 'tensor'))
- counts: int32 [128], P('dp'), may hold values from 1 to 3, as said below
- destination: int32 [512], P('dp'), may hold values from 0 to 127, as said below
- lengths: int32 [512], P('dp'), may hold values from 1 to 8
- labels: int32 [512, 8], P('dp'), may hold values from 0 to 152063
Outputs:
- scores: float32 [256], P('dp')
Inputs may be any that keep to these rules, and one draw needn't show every extreme that they name: The first counts[i] slots of index i are live; the counts sum to 256. The live slots of index i go to i or to i + 1, lower slots first to i; every index of dp is the destination of exactly 2 live slots; at most 1 live slots of one index go to the next index, a bound reached in every draw; entries of slots that are not live are arbitrary.
All inputs are finite; a program needn't handle non-finite values.
Results may differ from a plain program's by a relative error of at most 0.0025.
Values may be sent and summed in bfloat16 or wider, within the bound.
No kernel may reach another device: no remote copies, remote signals or barrier semaphores. Data moves between devices by JAX's collectives and lax.ppermute only.
A program may use at most 64 MiB of HBM per device.

v0:
```python
import jax
import jax.numpy as jnp
from jax import lax
from jax.sharding import Mesh
from jax.sharding import PartitionSpec as P

BLK_DEV = 2
DP = ("dp_0", "dp_1", "dp_2")
DP_TENSOR = ("dp_0", "dp_1", "dp_2", "tensor")


epsilon = 1e-06


def from_behind(block, axis, distance):
    devices = range(lax.axis_size(axis))
    route = [(i - distance, i) for i in devices if i - distance in devices]
    return lax.ppermute(block, axis, route)


def from_everyone(shard, axis):
    copies = jnp.broadcast_to(shard, (lax.axis_size(axis), *shard.shape))
    return lax.all_to_all(copies, axis, split_axis=0, concat_axis=0, tiled=True)


def in_order(tiles, dim):
    lengths = list(tiles.shape[1:])
    lengths[dim] *= tiles.shape[0]
    return jnp.moveaxis(tiles, 0, dim).reshape(lengths)


def collect(shard, axis, dim):
    tiles = from_everyone(shard, axis)
    return in_order(tiles, dim)


def by_axis(shard, axes):
    for axis in axes:
        shard = lax.pmax(shard, axis)
    return shard


def taken_together(shard, axis):
    return from_everyone(shard, axis).sum(axis=0)


def normalize(rows, norm_gain):
    values = rows.astype(jnp.float32)
    mean_square = jnp.mean(values * values, axis=-1, keepdims=True)
    return (values * lax.rsqrt(mean_square + epsilon) * norm_gain).astype(jnp.bfloat16)


def make_absorb(weight, vocab_start):

    def absorb(running, incoming, offset_row):
        rows, row_labels = incoming
        logits = lax.dot_general(
            rows, weight, (((1,), (1,)), ((), ())), preferred_element_type=jnp.float32
        )
        row_peak = jnp.max(logits, axis=1)
        scaled = jnp.exp(logits - row_peak[:, None])
        vocab_ids = vocab_start + jnp.arange(weight.shape[0], dtype=jnp.int32)
        hit = vocab_ids[None, :] == row_labels[:, None]
        fresh = (
            row_peak,
            jnp.sum(scaled, axis=1),
            jnp.sum(scaled * scaled, axis=1),
            jnp.sum(jnp.where(hit, logits, 0.0), axis=1),
        )
        return tuple((new for new in fresh))

    return absorb


def empty_stats(length):
    return tuple((jnp.zeros((length,), jnp.float32) for index in range(4)))


def earlier_count(flags):
    total = flags.shape[0]
    slot_ids = jnp.arange(total, dtype=jnp.int32)
    before = flags[None, :] & (slot_ids[None, :] < slot_ids[:, None])
    return jnp.sum(before, axis=1)


def per_device(hidden, norm_gain, head_weight, counts, destination, lengths, labels):
    capacity, block_len, quarter_width = hidden.shape
    peer_count = lax.axis_size(DP)
    tensor_ways = lax.axis_size("tensor")
    received_blocks = BLK_DEV
    spill_slots = BLK_DEV - 1
    dp_index = lax.axis_index(DP)
    tensor_index = lax.axis_index("tensor")
    slot_ids = jnp.arange(capacity, dtype=jnp.int32)
    is_live = slot_ids < counts[0]
    leaving = is_live & (destination == dp_index + 1)
    staying = is_live & (destination == dp_index)
    leave_rank = earlier_count(leaving)
    stay_rank = earlier_count(staying)
    flat_hidden = hidden.reshape(capacity, block_len * quarter_width)
    send_pick = (
        jnp.arange(spill_slots, dtype=jnp.int32)[:, None] == leave_rank[None, :]
    ) & leaving[None, :]
    packed = jnp.dot(
        send_pick.astype(jnp.bfloat16), flat_hidden, preferred_element_type=jnp.float32
    ).astype(jnp.bfloat16)
    packed_labels = jnp.sum(jnp.where(send_pick[:, :, None], labels[None, :, :], 0), axis=1)
    packed_lengths = jnp.sum(jnp.where(send_pick, lengths[None, :], 0), axis=1)
    occupied = jnp.sum(send_pick, axis=1)
    arrived, arrived_labels, arrived_lengths, arrived_occupied = from_behind(
        (packed, packed_labels, packed_lengths, occupied), DP, 1
    )
    incoming = jnp.sum(arrived_occupied).astype(jnp.int32)
    final_ids = jnp.arange(received_blocks, dtype=jnp.int32)
    place_in = (final_ids[:, None] == jnp.arange(spill_slots, dtype=jnp.int32)[None, :]) & (
        arrived_occupied > 0
    )[None, :]
    place_own = (final_ids[:, None] == (incoming + stay_rank)[None, :]) & staying[None, :]
    local = jnp.dot(place_in.astype(jnp.bfloat16), arrived, preferred_element_type=jnp.float32)
    local = local + jnp.dot(
        place_own.astype(jnp.bfloat16), flat_hidden, preferred_element_type=jnp.float32
    )
    local = local.astype(jnp.bfloat16).reshape(received_blocks * block_len, quarter_width)
    local_labels = jnp.sum(
        jnp.where(place_in[:, :, None], arrived_labels[None, :, :], 0), axis=1
    ) + jnp.sum(jnp.where(place_own[:, :, None], labels[None, :, :], 0), axis=1)
    local_labels = local_labels.reshape(-1).astype(jnp.int32)
    local_lengths = jnp.sum(jnp.where(place_in, arrived_lengths[None, :], 0), axis=1) + jnp.sum(
        jnp.where(place_own, lengths[None, :], 0), axis=1
    )
    local_lengths = local_lengths.astype(jnp.int32)
    token_count = received_blocks * block_len
    share = token_count // tensor_ways
    vocab_rows = head_weight.shape[0]
    gathered = collect(local, "tensor", 1)
    normed = normalize(gathered, norm_gain)
    absorb = make_absorb(head_weight, (dp_index * tensor_ways + tensor_index) * vocab_rows)
    row_peak, exp_sum, square_sum, label_logit = absorb(
        empty_stats(peer_count * token_count),
        (
            lax.all_gather(normed, DP, axis=0, tiled=True),
            lax.all_gather(local_labels, DP, axis=0, tiled=True),
        ),
        jnp.int32(0),
    )
    global_peak = by_axis(row_peak, DP_TENSOR)
    rescale = jnp.exp(row_peak - global_peak)
    exp_sum, square_sum, label_logit = (
        lax.psum_scatter(exp_sum * rescale, DP_TENSOR, scatter_dimension=0, tiled=True),
        lax.psum_scatter(
            square_sum * rescale * rescale, DP_TENSOR, scatter_dimension=0, tiled=True
        ),
        lax.psum_scatter(label_logit, DP_TENSOR, scatter_dimension=0, tiled=True),
    )
    own_peak = lax.dynamic_slice_in_dim(
        global_peak, (dp_index * tensor_ways + tensor_index) * share, share
    )
    token_error = (
        square_sum / (exp_sum * exp_sum) - 2.0 * jnp.exp(label_logit - own_peak) / exp_sum + 1.0
    )
    position = tensor_index * share + jnp.arange(share, dtype=jnp.int32)
    owner = (
        jnp.arange(received_blocks, dtype=jnp.int32)[:, None] == (position // block_len)[None, :]
    )
    token_length = jnp.sum(jnp.where(owner, local_lengths[:, None], 0), axis=0)
    counted = jnp.where(position % block_len < token_length, token_error, 0.0)
    partial_sum = jnp.sum(jnp.where(owner, counted[None, :], 0.0), axis=1)
    totals = taken_together(partial_sum, "tensor")
    return totals / local_lengths.astype(jnp.float32)


def solution(mesh):
    finer = Mesh(
        mesh.devices.reshape(8, 8, 2, mesh.shape["tensor"]), ("dp_0", "dp_1", "dp_2", "tensor")
    )
    placed = (P(DP, None, "tensor"), P(), P(DP_TENSOR, None), P(DP), P(DP), P(DP), P(DP, None))
    return jax.shard_map(per_device, mesh=finer, in_specs=placed, out_specs=P(DP), check_vma=False)
```

profile of v0, /device:TPU:1, one launch (start us, length us, event | category | flops | bytes accessed | tf_op | source)
XLA Modules:
  0.0 295.9 jit_solution(11436306540069125314)
XLA Ops:
  8.1 1.3 select_reduce_fusion.6
  9.4 4.6 %collective-permute-start = (s32[1]{0:T(128)}, s32[1]{0:T(128)}, u32[]{:S(2)}, u32[]{:S(2)}) collective-permute-start(s32[1]{0:T(128)} %bitcast.1), channel_id=1, source_target_pairs={{0,4},{4,8},{8,12},{12,16},{16,20},{20,24},{24,28},{28,32},{32,36}... | collective-permute-start | bytes 20 | tf_op jit(solution)/shard_map/ppermute | solution.py:18
  14.0 0.8 copy.14
  15.1 1.9 collective-permute-start.2
  17.1 1.3 collective-permute-done
  18.4 0.7 broadcast_add_fusion
  19.1 0.8 select_reduce_fusion.5
  21.4 7.1 %all_to_all.11 = bf16[4,16,896]{2,1,0:T(8,128)(2,1)S(1)} all-to-all(bf16[4,16,896]{2,1,0:T(8,128)(2,1)S(1)} %broadcast_in_dim.150), channel_id=1, replica_groups=mesh['dp_0'=8,'dp_1'=8,'dp_2'=2,'tensor'=4] {'tensor'}, dimensions={0} | all-to-all | bytes 229376 | tf_op jit(solution)/shard_map/all_to_all | solution.py:23
  28.7 1.4 multiply_convert_fusion
  30.2 0.8 select_reduce_fusion.2
  31.0 4.6 %collective-permute-start.3 = (s32[1,8]{1,0:T(1,128)S(1)}, s32[1,8]{1,0:T(1,128)S(1)}, u32[]{:S(2)}, u32[]{:S(2)}) collective-permute-start(s32[1,8]{1,0:T(1,128)S(1)} %bitcast.36), channel_id=1, source_target_pairs={{0,4},{4,8},{8,12},{12,16},{16,20},{20,24},{24,28},{28,32},{32,36}... | collective-permute-start | bytes 104 | tf_op jit(solution)/shard_map/ppermute | solution.py:18
  35.6 1.9 collective-permute-start.1
  37.5 1.3 dynamic-slice
  40.7 25.7 %all-reduce = s32[2048]{0:T(1024)S(1)} all-reduce(s32[2048]{0:T(1024)S(1)} %add_dynamic-update-slice_fusion), channel_id=1, replica_groups=mesh['dp_0'=8,'dp_1'=8,'dp_2'=2,'tensor'=4] {'dp_0','dp_1','dp_2'}, use_global_device_ids=true, to_apply=%add | all-reduce | flops 2048 | bytes 16384
  66.4 64.2 %all-gather.2.cloned.1.call-done = bf16[2048,3584]{1,0:T(8,128)(2,1)} async-done(((bf16[16,3584]{1,0:T(8,128)(2,1)}), bf16[2048,3584]{1,0:T(8,128)(2,1)}) %all-gather.2.cloned.1.call-update) | async-done | bytes 14680080 | tf_op jit(solution)/shard_map/all_gather | solution.py:141
  130.6 9.6 %fusion.9 = (f32[2048]{0:T(1024)S(1)}, f32[2048,297]{0,1:T(8,128)}) fusion(bf16[2048,3584]{1,0:T(8,128)(2,1)} %all-gather.2.cloned.1.call-done, bf16[297,3584]{1,0:T(8,128)(2,1)S(1)} %copy-done), kind=kOutput, calls=%fused_computation.51 | convolution fusion | flops 4360585216 | bytes 19250176 | tf_op jit(solution)/shard_map/dot_general | solution.py:57
  140.2 12.8 %pmax.28 = f32[2048]{0:T(1024)S(1)} all-reduce(f32[2048]{0:T(1024)S(1)} %get-tuple-element.20), channel_id=1, replica_groups=mesh['dp_0'=8,'dp_1'=8,'dp_2'=2,'tensor'=4] {'dp_0'}, use_global_device_ids=true, to_apply=%region_9.10 | all-reduce | flops 2048 | bytes 16384 | tf_op jit(solution)/shard_map/pmax | solution.py:39
  153.0 12.1 %pmax.29 = f32[2048]{0:T(1024)S(1)} all-reduce(f32[2048]{0:T(1024)S(1)} %pmax.28), channel_id=1, replica_groups=mesh['dp_0'=8,'dp_1'=8,'dp_2'=2,'tensor'=4] {'dp_1'}, use_global_device_ids=true, to_apply=%region_10.11 | all-reduce | flops 2048 | bytes 16384 | tf_op jit(solution)/shard_map/pmax | solution.py:39
  165.0 9.9 %pmax.30 = f32[2048]{0:T(1024)S(1)} all-reduce(f32[2048]{0:T(1024)S(1)} %pmax.29), channel_id=1, replica_groups=mesh['dp_0'=8,'dp_1'=8,'dp_2'=2,'tensor'=4] {'dp_2'}, use_global_device_ids=true, to_apply=%region_11.12 | all-reduce | flops 2048 | bytes 16384 | tf_op jit(solution)/shard_map/pmax | solution.py:39
  174.9 8.5 %pmax.31 = f32[2048]{0:T(1024)S(1)} all-reduce(f32[2048]{0:T(1024)S(1)} %pmax.30), channel_id=1, replica_groups=mesh['dp_0'=8,'dp_1'=8,'dp_2'=2,'tensor'=4] {'tensor'}, use_global_device_ids=true, to_apply=%region_12.13 | all-reduce | flops 2048 | bytes 16384 | tf_op jit(solution)/shard_map/pmax | solution.py:39
  183.4 2.5 fusion
  185.9 94.7 %all-reduce.4 = (f32[2048]{0:T(1024)S(1)}, f32[2048]{0:T(1024)S(1)}, f32[2048]{0:T(1024)S(1)}) all-reduce(f32[2048]{0:T(1024)S(1)} %get-tuple-element.7, f32[2048]{0:T(1024)S(1)} %get-tuple-element.17, f32[2048]{0:T(1024)S(1)} %get-tuple-element.16), channel_id=4, replica_groups=mesh['dp_0'=8,'dp_1'=8,'dp_2'=2,'tensor'=4] {'dp_0','dp_1','dp_2','tensor'}, use_global_device_ids=true, to_apply=%region_19.20.clone | all-reduce | flops 6144 | bytes 49152
  280.9 7.0 %all_to_all.12 = f32[4,1,2]{2,1,0:T(1,128)S(1)} all-to-all(f32[4,1,2]{2,1,0:T(1,128)S(1)} %broadcast_in_dim.163), channel_id=1, replica_groups=mesh['dp_0'=8,'dp_1'=8,'dp_2'=2,'tensor'=4] {'tensor'}, dimensions={0} | all-to-all | bytes 64 | tf_op jit(solution)/shard_map/all_to_all | solution.py:23
  287.9 1.2 convert_divide_fusion
  (40 shorter events, 3.5 us)
Async XLA Ops:
  6.5 124.1 %copy-start = (bf16[297,3584]{1,0:T(8,128)(2,1)S(1)}, bf16[297,3584]{1,0:T(8,128)(2,1)}, u32[]{:S(2)}) copy-start(bf16[297,3584]{1,0:T(8,128)(2,1)} %param.9) | copy-start | bytes 6386692
  6.5 33.0 %copy-start.1 = (s32[4,8]{1,0:T(4,128)S(1)}, s32[4,8]{1,0:T(4,128)}, u32[]{:S(2)}) copy-start(s32[4,8]{1,0:T(4,128)} %param.13) | copy-start | bytes 388
  6.5 124.1 %all-gather.2.cloned.1.call-start = ((), (), s32[]{:S(2)}) async-start(), calls=%async_computation.2 | async-start | bytes 14794752 | tf_op jit(solution)/shard_map/all_gather | solution.py:141
  9.4 8.9 %collective-permute-start = (s32[1]{0:T(128)}, s32[1]{0:T(128)}, u32[]{:S(2)}, u32[]{:S(2)}) collective-permute-start(s32[1]{0:T(128)} %bitcast.1), channel_id=1, source_target_pairs={{0,4},{4,8},{8,12},{12,16},{16,20},{20,24},{24,28},{28,32},{32,36}... | collective-permute-start | bytes 20 | tf_op jit(solution)/shard_map/ppermute | solution.py:18
  15.1 6.1 %collective-permute-start.2 = (bf16[1,7168]{1,0:T(2,128)(2,1)S(1)}, bf16[1,7168]{1,0:T(2,128)(2,1)S(1)}, u32[]{:S(2)}, u32[]{:S(2)}) collective-permute-start(bf16[1,7168]{1,0:T(2,128)(2,1)S(1)} %convert_element_type.45), channel_id=1, source_target_pairs={{0,4},{4,8},{8,12},{12,16},{16,20},{20,24},{24,28},{28,32},{32,36}... | collective-permute-start | bytes 43016 | tf_op jit(solution)/shard_map/ppermute | solution.py:18
  31.0 9.5 %collective-permute-start.3 = (s32[1,8]{1,0:T(1,128)S(1)}, s32[1,8]{1,0:T(1,128)S(1)}, u32[]{:S(2)}, u32[]{:S(2)}) collective-permute-start(s32[1,8]{1,0:T(1,128)S(1)} %bitcast.36), channel_id=1, source_target_pairs={{0,4},{4,8},{8,12},{12,16},{16,20},{20,24},{24,28},{28,32},{32,36}... | collective-permute-start | bytes 104 | tf_op jit(solution)/shard_map/ppermute | solution.py:18
  35.6 4.1 %collective-permute-start.1 = (s32[1]{0:T(128)}, s32[1]{0:T(128)}, u32[]{:S(2)}, u32[]{:S(2)}) collective-permute-start(s32[1]{0:T(128)} %bitcast.3), channel_id=1, source_target_pairs={{0,4},{4,8},{8,12},{12,16},{16,20},{20,24},{24,28},{28,32},{32,36}... | collective-permute-start | bytes 20 | tf_op jit(solution)/shard_map/ppermute | solution.py:18
Sparse Core Ops, SparseCore 0:
  30.3 100.2 all-gather.1
where the time goes:
time: 297 us; the launch traced here: 296 us
  blocking collectives  178 us (60%)
  waiting for transfers between devices  66.1 us (22%)
  between operations  15.8 us (5%)
  starting transfers between devices  13 us (4%)
  other arithmetic  11 us (4%)
  matrix products  9.88 us (3%)
    unnamed x2, blocking collectives  120 us
    all_gather x1, waiting for transfers between devices, per_device(): lax.all_gather(normed, DP, axis=0, tiled=True)  64.2 us
    pmax x4, blocking collectives, by_axis(): shard = lax.pmax(shard, axis)  43.2 us
    all_to_all x2, blocking collectives, from_everyone(): return lax.all_to_all(copies, axis, split_axis=0, concat_axis=0, tiled=True)  14.1 us
    ppermute x4, starting transfers between devices, from_behind(): return lax.ppermute(block, axis, route)  13 us
    dot_general x1, matrix products, absorb(): lax.dot_general(rows, weight, (((1,), (1,)), ((), ())), preferred_element...  9.57 us
  transfers between devices with their start and end apart: 5, of which 3 were waited for; matrix products, arithmetic and copies ran while one was open for 2% of the time, Pallas kernels for 0%

commit v1 on v0

v1 whole, which is shorter than its diff:
```python
import jax
import jax.numpy as jnp
from jax import lax
from jax.sharding import Mesh
from jax.sharding import PartitionSpec as P

BLK_DEV = 2
DP = ("dp_0", "dp_1", "dp_2")
DP_TENSOR = ("dp_0", "dp_1", "dp_2", "tensor")

GRID = (8, 8)
epsilon = 1e-06


def from_behind(block):
    devices = lax.axis_size(DP)
    return lax.ppermute(block, DP, [(i, i + 1) for i in range(devices - 1)])


def to_everyone(shard, axes):
    copies = jnp.broadcast_to(shard[None], (lax.axis_size(axes), *shard.shape))
    return lax.all_to_all(copies, axes, split_axis=0, concat_axis=0, tiled=True)


def received(stay, arrived, own):
    from_last = stay < BLK_DEV
    return jnp.where(
        from_last, jnp.stack([arrived, own[0]]), jnp.stack([own[0], own[1]])
    )


def normalize(rows, norm_gain):
    values = rows.astype(jnp.float32)
    mean_square = jnp.mean(values * values, axis=-1, keepdims=True)
    return (values * lax.rsqrt(mean_square + epsilon) * norm_gain).astype(jnp.bfloat16)


def per_device(hidden, norm_gain, head_weight, counts, destination, lengths, labels):
    capacity, block_len, quarter_width = hidden.shape
    dp_size = lax.axis_size(DP)
    tensor_ways = lax.axis_size("tensor")
    dp_index = lax.axis_index(DP)
    tensor_index = lax.axis_index("tensor")
    tokens = BLK_DEV * block_len
    is_live = jnp.arange(capacity, dtype=jnp.int32) < counts[0]
    stay = jnp.sum(is_live & (destination == dp_index)).astype(jnp.int32)
    stay = jnp.clip(stay, 1, BLK_DEV)
    leaving = jnp.where(stay == 1, hidden[1], hidden[2])
    facts = jnp.concatenate([labels, lengths[:, None]], axis=1)
    leaving_facts = jnp.where(stay == 1, facts[1], facts[2])
    arrived = from_behind(leaving)
    arrived_facts = from_behind(leaving_facts)
    local = received(stay, arrived, hidden).reshape(tokens, quarter_width)
    gathered = to_everyone(local, "tensor")
    gathered = jnp.moveaxis(gathered, 0, 1).reshape(tokens, tensor_ways * quarter_width)
    normed = normalize(gathered, norm_gain)
    local_facts = received(stay, arrived_facts, facts)
    local_labels = local_facts[:, :block_len].reshape(tokens)
    local_lengths = local_facts[:, block_len]

    rows = lax.all_gather(normed, DP, axis=0, tiled=True)
    row_labels = lax.all_gather(local_labels, DP, axis=0, tiled=True)
    vocab_rows = head_weight.shape[0]
    vocab_start = (dp_index * tensor_ways + tensor_index) * vocab_rows
    logits = lax.dot_general(
        rows, head_weight, (((1,), (1,)), ((), ())), preferred_element_type=jnp.float32
    )
    row_peak = jnp.max(logits, axis=1)
    scaled = jnp.exp(logits - row_peak[:, None])
    vocab_ids = vocab_start + jnp.arange(vocab_rows, dtype=jnp.int32)
    hit = vocab_ids[None, :] == row_labels[:, None]
    stats = jnp.stack(
        [
            row_peak.reshape(dp_size, tokens),
            jnp.sum(scaled, axis=1).reshape(dp_size, tokens),
            jnp.sum(scaled * scaled, axis=1).reshape(dp_size, tokens),
            jnp.sum(jnp.where(hit, logits, 0.0), axis=1).reshape(dp_size, tokens),
        ],
        axis=1,
    ).reshape(dp_size, 1, 4 * tokens)
    outgoing = jnp.broadcast_to(stats, (dp_size, tensor_ways, 4 * tokens))
    parts = lax.all_to_all(
        outgoing.reshape(dp_size * tensor_ways, 4 * tokens),
        DP_TENSOR,
        split_axis=0,
        concat_axis=0,
        tiled=True,
    )
    part_peak = parts[:, :tokens]
    peak = jnp.max(part_peak, axis=0)
    rescale = jnp.exp(part_peak - peak[None, :])
    exp_sum = jnp.sum(parts[:, tokens : 2 * tokens] * rescale, axis=0)
    square_sum = jnp.sum(parts[:, 2 * tokens : 3 * tokens] * rescale * rescale, axis=0)
    label_logit = jnp.sum(parts[:, 3 * tokens :], axis=0)
    token_error = (
        square_sum / (exp_sum * exp_sum) - 2.0 * jnp.exp(label_logit - peak) / exp_sum + 1.0
    ).reshape(BLK_DEV, block_len)
    valid = jnp.arange(block_len, dtype=jnp.int32)[None, :] < local_lengths[:, None]
    return jnp.sum(jnp.where(valid, token_error, 0.0), axis=1) / local_lengths.astype(jnp.float32)


def solution(mesh):
    dp, tensor = mesh.shape["dp"], mesh.shape["tensor"]
    finer = Mesh(mesh.devices.reshape(*GRID, dp // (GRID[0] * GRID[1]), tensor), DP_TENSOR)
    placed = (P(DP, None, "tensor"), P(), P(DP_TENSOR, None), P(DP), P(DP), P(DP), P(DP, None))
    return jax.shard_map(per_device, mesh=finer, in_specs=placed, out_specs=P(DP), check_vma=False)
```

time: 297 us -> 181 us (0.61)
  blocking collectives: 178 us -> 34 us
  waiting for transfers between devices: 66.1 us -> 86.4 us
  starting transfers between devices: 13 us -> 21.9 us
    unnamed x2 -> x1, blocking collectives: 120 us -> 26.9 us
    pmax x4 -> x0, blocking collectives: 43.2 us -> none  [by_axis(): shard = lax.pmax(shard, axis)]
    all_to_all x0 -> x1, waiting for transfers between devices: none -> 16.3 us  [per_device(): lax.all_to_all(outgoing.reshape(dp_size * tensor_ways, 4 * tokens), DP_TE...]
    all_to_all x0 -> x1, starting transfers between devices: none -> 13.7 us  [per_device(): lax.all_to_all(outgoing.reshape(dp_size * tensor_ways, 4 * tokens), DP_TE...]
    all_to_all x2 -> x1, blocking collectives: 14.1 us -> 7.15 us  [to_everyone(): return lax.all_to_all(copies, axes, split_axis=0, concat_axis=0, tiled=True)]
    ppermute x4 -> x2, starting transfers between devices: 13 us -> 8.22 us  [from_behind(): return lax.ppermute(block, DP, [(i, i + 1) for i in range(devices - 1)])]
    dot_general x3 -> x1, matrix products: 9.88 us -> 9.57 us  [per_device(): lax.dot_general(rows, head_weight, (((1,), (1,)), ((), ())), preferred_el...]
  transfers between devices with their start and end apart: 5 -> 4, of which waited for: 3 -> 3; matrix products, arithmetic and copies ran while one was open for 2% -> 2% of each run, Pallas kernels for 0% -> 0%
where the time goes in v1:
time: 181 us
  waiting for transfers between devices  86.4 us (48%)
  blocking collectives  34 us (19%)
  starting transfers between devices  21.9 us (12%)
  between operations  15.7 us (9%)
  matrix products  9.57 us (5%)
  other arithmetic  8.87 us (5%)
  local copies, waits for them, and re-layouts  4.04 us (2%)
    all_gather x1, waiting for transfers between devices, per_device(): rows = lax.all_gather(normed, DP, axis=0, tiled=True)  66 us
    unnamed x1, blocking collectives  26.9 us
    all_to_all x1, waiting for transfers between devices, per_device(): lax.all_to_all(outgoing.reshape(dp_size * tensor_ways, 4 * tokens), DP_TE...  16.3 us
    all_to_all x1, starting transfers between devices, per_device(): lax.all_to_all(outgoing.reshape(dp_size * tensor_ways, 4 * tokens), DP_TE...  13.7 us
    dot_general x1, matrix products, per_device(): lax.dot_general(rows, head_weight, (((1,), (1,)), ((), ())), preferred_el...  9.57 us
    ppermute x2, starting transfers between devices, from_behind(): return lax.ppermute(block, DP, [(i, i + 1) for i in range(devices - 1)])  8.22 us
    all_to_all x1, blocking collectives, to_everyone(): return lax.all_to_all(copies, axes, split_axis=0, concat_axis=0, tiled=True)  7.15 us
    ppermute x2, waiting for transfers between devices, from_behind(): return lax.ppermute(block, DP, [(i, i + 1) for i in range(devices - 1)])  4.2 us
  transfers between devices with their start and end apart: 4, of which 3 were waited for; matrix products, arithmetic and copies ran while one was open for 2% of the time, Pallas kernels for 0%

profile of v1, /device:TPU:1, one launch (start us, length us, event | category | flops | bytes accessed | tf_op | source)
XLA Modules:
  0.0 180.5 jit_solution(2270608980672060785)
XLA Ops:
  7.3 1.4 fusion.7
  9.4 0.8 select_bitcast_fusion
  10.2 4.6 %collective-permute-start.1 = (bf16[8,896]{1,0:T(8,128)(2,1)S(1)}, bf16[8,896]{1,0:T(8,128)(2,1)S(1)}, u32[]{:S(2)}, u32[]{:S(2)}) collective-permute-start(bf16[8,896]{1,0:T(8,128)(2,1)S(1)} %get-tuple-element.11), channel_id=1, source_target_pairs={{0,4},{4,8},{8,12},{12,16},{16,20},{20,24},{24,28},{28,32},{32,36}... | collective-permute-start | bytes 43016 | tf_op jit(solution)/shard_map/ppermute | solution.py:17
  14.8 4.2 %collective-permute-done.1 = bf16[8,896]{1,0:T(8,128)(2,1)S(1)} collective-permute-done((bf16[8,896]{1,0:T(8,128)(2,1)S(1)}, bf16[8,896]{1,0:T(8,128)(2,1)S(1)}, u32[]{:S(2)}, u32[]{:S(2)}) %collective-permute-start.1) | collective-permute-done | bytes 14368 | tf_op jit(solution)/shard_map/ppermute | solution.py:17
  19.0 0.8 fusion.4
  19.7 7.1 %all_to_all.17 = bf16[4,16,896]{2,1,0:T(8,128)(2,1)S(1)} all-to-all(bf16[4,16,896]{2,1,0:T(8,128)(2,1)S(1)} %broadcast_in_dim.34), channel_id=1, replica_groups=mesh['dp_0'=8,'dp_1'=8,'dp_2'=2,'tensor'=4] {'tensor'}, dimensions={0} | all-to-all | bytes 229376 | tf_op jit(solution)/shard_map/all_to_all | solution.py:22
  26.9 0.1 fusion.3
  27.1 1.4 multiply_convert_fusion
  28.5 0.7 copy.12
  29.3 0.8 pad_add_fusion
  30.0 3.7 %collective-permute-start = (s32[9]{0:T(128)S(1)}, s32[9]{0:T(128)S(1)}, u32[]{:S(2)}, u32[]{:S(2)}) collective-permute-start(s32[9]{0:T(128)S(1)} %get-tuple-element.13), channel_id=1, source_target_pairs={{0,4},{4,8},{8,12},{12,16},{16,20},{20,24},{24,28},{28,32},{32,36}... | collective-permute-start | bytes 116 | tf_op jit(solution)/shard_map/ppermute | solution.py:17
  33.7 1.3 dynamic-slice
  35.8 0.2 dynamic-update-slice
  36.0 26.9 %all-reduce = s32[2048]{0:T(1024)S(1)} all-reduce(s32[2048]{0:T(1024)S(1)} %dynamic-update-slice), channel_id=1, replica_groups=mesh['dp_0'=8,'dp_1'=8,'dp_2'=2,'tensor'=4] {'dp_0','dp_1','dp_2'}, use_global_device_ids=true, to_apply=%add | all-reduce | flops 2048 | bytes 16384
  62.8 66.0 %all-gather.2.cloned.1.call-done = bf16[2048,3584]{1,0:T(8,128)(2,1)} async-done(((bf16[16,3584]{1,0:T(8,128)(2,1)}), bf16[2048,3584]{1,0:T(8,128)(2,1)}) %all-gather.2.cloned.1.call-update) | async-done | bytes 14680080 | tf_op jit(solution)/shard_map/all_gather | solution.py:61
  128.8 9.6 %fusion.8 = (f32[2048]{0:T(1024)S(1)}, f32[2048,297]{0,1:T(8,128)}) fusion(bf16[2048,3584]{1,0:T(8,128)(2,1)} %all-gather.2.cloned.1.call-done, bf16[297,3584]{1,0:T(8,128)(2,1)S(1)} %copy-done), kind=kOutput, calls=%fused_computation.32 | convolution fusion | flops 4360585216 | bytes 19250176 | tf_op jit(solution)/shard_map/dot_general | solution.py:65
  138.5 2.5 %fusion = (f32[2048]{0:T(1024)S(1)}, f32[2048]{0:T(1024)S(1)}, f32[2048]{0:T(1024)S(1)}) fusion(f32[2048,297]{0,1:T(8,128)} %get-tuple-element.16, f32[2048]{0:T(1024)S(1)} %get-tuple-element.15, s32[2048]{0:T(1024)S(1)} %all-reduce, s32[297]{0:T(512)S(1)} %iota_add_fusion), kind=kLoop, calls=%fused_computation.3 | loop fusion | flops 4251648 | bytes 2475172 | tf_op jit(solution)/shard_map/reduce_sum | solution.py:75
  141.6 0.7 broadcast_in_dim.37
  142.3 13.7 %all-to-all-start.1 = ((f32[512,1,64]{2,1,0:T(1,128)}), f32[512,1,64]{2,1,0:T(1,128)S(1)}, u32[]{:S(2)}, u32[]{:S(2)}) async-start(f32[512,1,64]{2,1,0:T(1,128)} %bitcast.10), calls=%async_computation.1 | async-start | bytes 524288 | tf_op jit(solution)/shard_map/all_to_all | solution.py:82
  156.1 0.2 slice_reduce_fusion.2
  156.2 16.3 %all-to-all-done.1 = f32[512,1,64]{2,1,0:T(1,128)S(1)} async-done(((f32[512,1,64]{2,1,0:T(1,128)}), f32[512,1,64]{2,1,0:T(1,128)S(1)}, u32[]{:S(2)}, u32[]{:S(2)}) %all-to-all-start.1) | async-done | bytes 131104 | tf_op jit(solution)/shard_map/all_to_all | solution.py:82
  172.6 0.3 fusion.2
  173.0 0.2 fusion.5
  173.1 0.5 convert_divide_fusion
  (27 shorter events, 1.1 us)
Async XLA Ops:
  6.5 122.3 %copy-start = (bf16[297,3584]{1,0:T(8,128)(2,1)S(1)}, bf16[297,3584]{1,0:T(8,128)(2,1)}, u32[]{:S(2)}) copy-start(bf16[297,3584]{1,0:T(8,128)(2,1)} %param.9) | copy-start | bytes 6386692
  6.5 122.3 %all-gather.2.cloned.1.call-start = ((), (), s32[]{:S(2)}) async-start(), calls=%async_computation.2 | async-start | bytes 14794752 | tf_op jit(solution)/shard_map/all_gather | solution.py:61
  10.2 8.8 %collective-permute-start.1 = (bf16[8,896]{1,0:T(8,128)(2,1)S(1)}, bf16[8,896]{1,0:T(8,128)(2,1)S(1)}, u32[]{:S(2)}, u32[]{:S(2)}) collective-permute-start(bf16[8,896]{1,0:T(8,128)(2,1)S(1)} %get-tuple-element.11), channel_id=1, source_target_pairs={{0,4},{4,8},{8,12},{12,16},{16,20},{20,24},{24,28},{28,32},{32,36}... | collective-permute-start | bytes 43016 | tf_op jit(solution)/shard_map/ppermute | solution.py:17
  30.0 5.6 %collective-permute-start = (s32[9]{0:T(128)S(1)}, s32[9]{0:T(128)S(1)}, u32[]{:S(2)}, u32[]{:S(2)}) collective-permute-start(s32[9]{0:T(128)S(1)} %get-tuple-element.13), channel_id=1, source_target_pairs={{0,4},{4,8},{8,12},{12,16},{16,20},{20,24},{24,28},{28,32},{32,36}... | collective-permute-start | bytes 116 | tf_op jit(solution)/shard_map/ppermute | solution.py:17
  142.3 30.2 %all-to-all-start.1 = ((f32[512,1,64]{2,1,0:T(1,128)}), f32[512,1,64]{2,1,0:T(1,128)S(1)}, u32[]{:S(2)}, u32[]{:S(2)}) async-start(f32[512,1,64]{2,1,0:T(1,128)} %bitcast.10), calls=%async_computation.1 | async-start | bytes 524288 | tf_op jit(solution)/shard_map/all_to_all | solution.py:82
Sparse Core Ops, SparseCore 0:
  28.7 100.0 all-gather.1

commit v2 on v1

v2 whole, which is shorter than its diff:
```python
import functools

import jax
import jax.numpy as jnp
from jax import lax
from jax.experimental import pallas as pl
from jax.experimental.pallas import tpu as pltpu
from jax.sharding import Mesh
from jax.sharding import PartitionSpec as P


BLK_DEV = 2
DP = ("dp_0", "dp_1", "dp_2")
PLANE = ("dp_0", "dp_1")
SPACE = ("dp_0", "dp_1", "tensor")
DP_TENSOR = ("dp_0", "dp_1", "dp_2", "tensor")

GRID = (8, 8)
INTERPRET = False
epsilon = 1e-06
NOTES = 128
STATS = 4


def around(block, axis, step):
    size = lax.axis_size(axis)
    return lax.ppermute(block, axis, [(i, (i + step) % size) for i in range(size)])


def from_behind(block):
    devices = lax.axis_size(DP)
    return lax.ppermute(block, DP, [(i, i + 1) for i in range(devices - 1)])


def exchange(pieces, axes):
    return lax.all_to_all(pieces, axes, split_axis=0, concat_axis=0, tiled=True)


def to_everyone(shard, axes):
    return exchange(jnp.broadcast_to(shard[None], (lax.axis_size(axes), *shard.shape)), axes)


def arrange_body(per_source, received, tokens, notes):
    ways, _, width = tokens.shape
    group = min(256, received.shape[0])
    share = group // ways
    row = lax.broadcasted_iota(jnp.int32, (group, group), 0)
    column = lax.broadcasted_iota(jnp.int32, (group, group), 1)
    token = row % share
    wanted = token // per_source * (ways * per_source) + token % per_source
    wanted = wanted + row // share * per_source
    pick = jnp.where(column == wanted, 1.0, 0.0).astype(jnp.bfloat16)
    for block in range(received.shape[0] // group):
        rows = received[block * group : (block + 1) * group, :]
        placed = jnp.dot(pick, rows, preferred_element_type=jnp.float32).astype(jnp.bfloat16)
        here = slice(block * share, (block + 1) * share)
        for q in range(ways):
            tokens[q, here, :] = placed[q * share : (q + 1) * share, :width]
        notes[here, :] = placed[:share, width:]


def arranged(received, ways, per_source, width):
    vmem = pl.BlockSpec(memory_space=pltpu.VMEM)
    count = received.shape[0] // ways
    return pl.pallas_call(
        functools.partial(arrange_body, per_source),
        out_shape=(
            jax.ShapeDtypeStruct((ways, count, width), jnp.bfloat16),
            jax.ShapeDtypeStruct((count, NOTES), jnp.bfloat16),
        ),
        in_specs=[vmem],
        out_specs=(vmem, vmem),
        interpret=INTERPRET,
        compiler_params=pltpu.CompilerParams(vmem_limit_bytes=16 * 1024 * 1024),
    )(received)


def absorb_body(layout, vocab_rows, starts, tokens, notes, carried, *refs):
    pieces = sum(len(rows) for rows in layout)
    sources, stats, held, arrival = refs[:pieces], refs[pieces], refs[pieces + 1 : -1], refs[-1]
    copies = []
    for chunk, rows in enumerate(layout):
        at = 0
        for size in rows:
            index = len(copies)
            target = held[chunk] if len(rows) == 1 else held[chunk].at[pl.ds(at, size)]
            copies.append(pltpu.make_async_copy(sources[index], target, arrival.at[index]))
            at += size
    for copy in copies:
        copy.start()
    quarters, _, width = tokens.shape
    lane = lax.broadcasted_iota(jnp.int32, (8, NOTES), 1)
    powers = jnp.where(lane == 0, 1.0, jnp.where(lane == 1, 256.0, 65536.0))
    powers = jnp.where(lane < 3, powers, 0.0).astype(jnp.bfloat16)
    labels = lax.dot_general(
        powers, notes[...], (((1,), (1,)), ((), ())), preferred_element_type=jnp.float32
    )[0:1].astype(jnp.int32)
    peak, exp_sum, square_sum, label_logit = (carried[i : i + 1, :] for i in range(STATS))
    waiting = iter(copies)
    for chunk, rows in enumerate(layout):
        for _ in rows:
            next(waiting).wait()
        logits = sum(
            lax.dot_general(
                held[chunk][:, q * width : (q + 1) * width],
                tokens[q],
                (((1,), (1,)), ((), ())),
                preferred_element_type=jnp.float32,
            )
            for q in range(quarters)
        )
        ids = lax.broadcasted_iota(jnp.int32, logits.shape, 0)
        if sum(rows) > vocab_rows:
            logits = jnp.where(ids < vocab_rows, logits, -jnp.inf)
        new_peak = jnp.maximum(peak, jnp.max(logits, axis=0, keepdims=True))
        rescale = jnp.exp(peak - new_peak)
        scaled = jnp.exp(logits - new_peak)
        hit = ids == labels - starts[chunk]
        exp_sum = exp_sum * rescale + jnp.sum(scaled, axis=0, keepdims=True)
        square_sum = square_sum * (rescale * rescale) + jnp.sum(
            scaled * scaled, axis=0, keepdims=True
        )
        label_logit = label_logit + jnp.sum(jnp.where(hit & (ids < vocab_rows), logits, 0.0), axis=0, keepdims=True)
        peak = new_peak
    stats[0:1, :] = peak
    stats[1:2, :] = exp_sum
    stats[2:3, :] = square_sum
    stats[3:4, :] = label_logit
    stats[4:8, :] = jnp.zeros((4, stats.shape[1]), jnp.float32)


def absorbed(carried, tokens, notes, chunks, vocab_rows):
    starts = jnp.stack([start for start, _ in chunks])
    pieces = [piece for _, held in chunks for piece in held]
    layout = [[piece.shape[0] for piece in held] for _, held in chunks]
    depth = pieces[0].shape[1]
    rows = sum(piece.shape[0] for piece in pieces)
    vmem = pl.BlockSpec(memory_space=pltpu.VMEM)
    return pl.pallas_call(
        functools.partial(absorb_body, layout, vocab_rows),
        out_shape=jax.ShapeDtypeStruct(carried.shape, jnp.float32),
        in_specs=[pl.BlockSpec(memory_space=pltpu.SMEM), vmem, vmem, vmem]
        + [pl.BlockSpec(memory_space=pl.ANY)] * len(pieces),
        out_specs=vmem,
        scratch_shapes=[pltpu.VMEM((sum(rows), depth), jnp.bfloat16) for rows in layout]
        + [pltpu.SemaphoreType.DMA((len(pieces),))],
        interpret=INTERPRET,
        cost_estimate=pl.CostEstimate(
            flops=2 * rows * tokens.size,
            bytes_accessed=2 * rows * depth,
            transcendentals=rows * tokens.shape[1],
        ),
        compiler_params=pltpu.CompilerParams(vmem_limit_bytes=32 * 1024 * 1024),
    )(starts, tokens, notes, carried, *pieces)


def per_device(hidden, norm_gain, head_weight, counts, destination, lengths, labels):
    capacity, block_len, width = hidden.shape
    ways = lax.axis_size("tensor")
    plane = lax.axis_size(PLANE)
    dp_index = lax.axis_index(DP)
    core_index = lax.axis_index("dp_2")
    tensor_index = lax.axis_index("tensor")
    share = BLK_DEV * block_len // ways
    cuts = block_len // share

    is_live = jnp.arange(capacity, dtype=jnp.int32) < counts[0]
    stay = jnp.sum(is_live & (destination == dp_index)).astype(jnp.int32)
    short = stay < BLK_DEV

    def placed(slots):
        own = jnp.stack([slots[0], jnp.where(short, slots[0], slots[1])])
        leaving = jnp.where(short, slots[1], slots[2])
        return own, leaving

    own, leaving = placed(hidden)
    own = own.reshape(ways, share, width)
    leaving = jnp.tile(leaving.reshape(cuts, share, width), (ways // cuts, 1, 1))
    gathered = exchange(jnp.concatenate([own, leaving], axis=1), "tensor")

    facts = jnp.stack(
        [labels % 256, labels // 256 % 256, labels // 65536]
        + [jnp.broadcast_to(lengths[:, None], labels.shape)],
        axis=-1,
    )
    own_facts, leaving_facts = placed(facts)
    own_lengths = own_facts[:, 0, 3]
    own_facts = lax.dynamic_index_in_dim(
        own_facts.reshape(ways, share, 4), tensor_index, keepdims=False
    )
    leaving_facts = lax.dynamic_index_in_dim(
        leaving_facts.reshape(cuts, share, 4), tensor_index % cuts, keepdims=False
    )
    notes = jnp.concatenate([own_facts, leaving_facts], axis=0).astype(jnp.bfloat16)

    vocab_rows = head_weight.shape[0]
    half = vocab_rows // 2 // 16 * 16
    top, bottom = head_weight[:half], jnp.pad(head_weight[half:], ((0, -vocab_rows % 16), (0, 0)))
    top, bottom, gathered = lax.optimization_barrier((top, bottom, gathered))
    low_top = around(top, "tensor", 1)
    high_bottom = around(bottom, "tensor", -1)

    values = gathered.astype(jnp.float32)
    mean_square = jnp.sum(values * values, axis=(0, 2), keepdims=True) / (ways * width)
    gain = norm_gain.reshape(ways, 1, width)
    normed = (values * lax.rsqrt(mean_square + epsilon) * gain).astype(jnp.bfloat16)
    notes = jnp.pad(notes[None], ((0, ways - 1), (0, 0), (0, NOTES - 4)))
    rows = jnp.concatenate([normed, notes], axis=2)
    arrived = from_behind(rows[:, share:])
    first = tensor_index < cuts
    message = jnp.where(short & first, arrived, rows[:, :share])
    arrived_length = arrived[0, 0, width + 3].astype(jnp.int32)
    local_lengths = jnp.stack([jnp.where(short, arrived_length, own_lengths[0]), own_lengths[1]])

    received = to_everyone(message.reshape(ways * share, width + NOTES), PLANE)
    low_bottom = around(bottom, "tensor", 1)
    high_top = around(top, "tensor", -1)
    far_top = around(low_top, "tensor", 1)
    far_bottom = around(high_bottom, "tensor", -1)

    partner = 1 - core_index
    chip = (lax.axis_index("dp_0") * lax.axis_size("dp_1") + lax.axis_index("dp_1")) * 2

    def start_of(core, step):
        return ((chip + core) * ways + (tensor_index + step) % ways) * vocab_rows

    held = ((0, (head_weight,)), (-1, (low_top, low_bottom)), (1, (high_top, high_bottom)))
    far = (far_top, far_bottom)
    near = [(start_of(core_index, step), pieces) for step, pieces in held]
    near += [
        (start_of(partner, step), [around(piece, "dp_2", 1) for piece in pieces])
        for step, pieces in held
    ]
    own_far = [(start_of(core_index, 2), far)]
    other_far = [(start_of(partner, 2), [around(piece, "dp_2", 1) for piece in far])]

    received = received.reshape(plane * ways * share, width + NOTES)
    tokens, token_notes = arranged(received, ways, share, width)
    empty = jnp.concatenate(
        [
            jnp.full((1, plane * share), -jnp.inf, jnp.float32),
            jnp.zeros((7, plane * share), jnp.float32),
        ]
    )
    stats = absorbed(empty, tokens, token_notes, near, vocab_rows)
    stats = absorbed(stats, tokens, token_notes, own_far, vocab_rows)
    stats = absorbed(stats, tokens, token_notes, other_far, vocab_rows)

    stats = jnp.moveaxis(stats[:STATS].reshape(STATS, plane, share), 1, 0)
    outgoing = jnp.broadcast_to(
        stats.reshape(plane, 1, STATS * share), (plane, ways, STATS * share)
    )
    sums = exchange(outgoing.reshape(plane * ways, STATS * share), SPACE)
    sums = sums.reshape(plane, ways, STATS * share)
    part_peak = sums[..., :share]
    peak = jnp.max(part_peak, axis=0)
    rescale = jnp.exp(part_peak - peak[None])
    exp_sum = jnp.sum(sums[..., share : 2 * share] * rescale, axis=0)
    square_sum = jnp.sum(sums[..., 2 * share : 3 * share] * rescale * rescale, axis=0)
    label_logit = jnp.sum(sums[..., 3 * share :], axis=0)
    token_error = (
        square_sum / (exp_sum * exp_sum) - 2.0 * jnp.exp(label_logit - peak) / exp_sum + 1.0
    ).reshape(BLK_DEV, block_len)
    valid = jnp.arange(block_len, dtype=jnp.int32)[None, :] < local_lengths[:, None]
    return jnp.sum(jnp.where(valid, token_error, 0.0), axis=1) / local_lengths.astype(jnp.float32)


def solution(mesh):
    dp, tensor = mesh.shape["dp"], mesh.shape["tensor"]
    finer = Mesh(mesh.devices.reshape(*GRID, dp // (GRID[0] * GRID[1]), tensor), DP_TENSOR)
    placed = (P(DP, None, "tensor"), P(), P(DP_TENSOR, None), P(DP), P(DP), P(DP), P(DP, None))
    return jax.shard_map(per_device, mesh=finer, in_specs=placed, out_specs=P(DP), check_vma=False)
```

time: 181 us -> 180 us (level)
  starting transfers between devices: 21.9 us -> 91.5 us
  waiting for transfers between devices: 86.4 us -> 44.7 us
  blocking collectives: 34 us -> 0 us
  Pallas kernels: 0 us -> 19 us
  between operations: 15.7 us -> 2.55 us
  local copies, waits for them, and re-layouts: 4.04 us -> 14.9 us
  matrix products: 9.57 us -> 0 us
  other arithmetic: 8.87 us -> 6.18 us
    all_gather x1 -> x0, waiting for transfers between devices: 66 us -> none  [per_device(): rows = lax.all_gather(normed, DP, axis=0, tiled=True)]
    ppermute x0 -> x13, starting transfers between devices: none -> 51.2 us  [around(): lax.ppermute(block, axis, [(i, (i + step) % size) for i in range(size)])]
    ppermute x0 -> x13, waiting for transfers between devices: none -> 30.2 us  [around(): lax.ppermute(block, axis, [(i, (i + step) % size) for i in range(size)])]
    unnamed x1 -> x0, blocking collectives: 26.9 us -> none
    all_to_all x1 -> x3, starting transfers between devices: 13.7 us -> 36.1 us  [exchange(): return lax.all_to_all(pieces, axes, split_axis=0, concat_axis=0, tiled=True)]
    pallas_call x0 -> x4, Pallas kernels: none -> 19 us  [the longest x3 16.6 us: absorbed(): pl.pallas_call(functools.partial(absorb_body, layout, vocab_rows), out_sh...]
    dot_general x1 -> x0, matrix products: 9.57 us -> none  [per_device(): lax.dot_general(rows, head_weight, (((1,), (1,)), ((), ())), preferred_el...]
    all_to_all x1 -> x0, blocking collectives: 7.15 us -> none  [to_everyone(): return lax.all_to_all(copies, axes, split_axis=0, concat_axis=0, tiled=True)]
  transfers between devices with their start and end apart: 4 -> 17, of which waited for: 3 -> 5; matrix products, arithmetic and copies ran while one was open for 2% -> 3% of each run, Pallas kernels for 0% -> 9%
where the time goes in v2:
time: 180 us; the launch traced here: 179 us
  starting transfers between devices  91.5 us (51%)
  waiting for transfers between devices  44.7 us (25%)
  Pallas kernels  19 us (11%)
  local copies, waits for them, and re-layouts  14.9 us (8%)
  other arithmetic  6.18 us (3%)
  between operations  2.55 us (1%)
    ppermute x13, starting transfers between devices, around(): lax.ppermute(block, axis, [(i, (i + step) % size) for i in range(size)])  51.2 us
    all_to_all x3, starting transfers between devices, exchange(): return lax.all_to_all(pieces, axes, split_axis=0, concat_axis=0, tiled=True)  36.1 us
    ppermute x13, waiting for transfers between devices, around(): lax.ppermute(block, axis, [(i, (i + step) % size) for i in range(size)])  30.2 us
    pallas_call x3, Pallas kernels, absorbed(): pl.pallas_call(functools.partial(absorb_body, layout, vocab_rows), out_sh...  16.6 us
    all_to_all x3, waiting for transfers between devices, exchange(): return lax.all_to_all(pieces, axes, split_axis=0, concat_axis=0, tiled=True)  11.4 us
    unnamed x25, local copies, waits for them, and re-layouts  7.06 us
    ppermute x1, starting transfers between devices, from_behind(): return lax.ppermute(block, DP, [(i, i + 1) for i in range(devices - 1)])  4.2 us
  transfers between devices with their start and end apart: 17, of which 5 were waited for; matrix products, arithmetic and copies ran while one was open for 3% of the time, Pallas kernels for 9%

profile of v2, /device:TPU:1, one launch (start us, length us, event | category | flops | bytes accessed | tf_op | source)
XLA Modules:
  0.0 178.9 jit_solution(16367567838708925788)
XLA Ops:
  4.1 4.8 %all-to-all-start = ((bf16[4,8,896]{2,1,0:T(8,128)(2,1)}), bf16[4,8,896]{2,1,0:T(8,128)(2,1)S(1)}, u32[]{:S(2)}, u32[]{:S(2)}) async-start(bf16[4,8,896]{2,1,0:T(8,128)(2,1)} %pad_maximum_fusion), calls=%async_computation | async-start | bytes 114688 | tf_op jit(solution)/shard_map/all_to_all | solution.py:36
  14.6 4.2 %collective-permute-start = (bf16[4,4,1024]{2,1,0:T(4,128)(2,1)S(1)}, bf16[4,4,1024]{2,1,0:T(4,128)(2,1)S(1)}, u32[]{:S(2)}, u32[]{:S(2)}) collective-permute-start(bf16[4,4,1024]{2,1,0:T(4,128)(2,1)S(1)} %slice.89), channel_id=1, source_target_pairs={{0,4},{4,8},{8,12},{12,16},{16,20},{20,24},{24,28},{28,32},{32,36}... | collective-permute-start | bytes 98312 | tf_op jit(solution)/shard_map/ppermute | solution.py:32
  18.9 3.2 %collective-permute-done = bf16[4,4,1024]{2,1,0:T(4,128)(2,1)S(1)} collective-permute-done((bf16[4,4,1024]{2,1,0:T(4,128)(2,1)S(1)}, bf16[4,4,1024]{2,1,0:T(4,128)(2,1)S(1)}, u32[]{:S(2)}, u32[]{:S(2)}) %collective-permute-start) | collective-permute-done | bytes 32800 | tf_op jit(solution)/shard_map/ppermute | solution.py:32
  23.7 13.6 %all-to-all-start.1 = ((bf16[64,16,1024]{2,1,0:T(8,128)(2,1)}), bf16[64,16,1024]{2,1,0:T(8,128)(2,1)}, u32[]{:S(2)}, u32[]{:S(2)}) async-start(bf16[64,16,1024]{2,1,0:T(8,128)(2,1)} %broadcast_in_dim.12), calls=%async_computation.1 | async-start | bytes 4194304 | tf_op jit(solution)/shard_map/all_to_all | solution.py:36
  37.3 3.5 %collective-permute-start.1 = (bf16[144,3584]{1,0:T(8,128)(2,1)S(1)}, bf16[144,3584]{1,0:T(8,128)(2,1)S(1)}, u32[]{:S(2)}, u32[]{:S(2)}) collective-permute-start(bf16[144,3584]{1,0:T(8,128)(2,1)S(1)} %slice.70), channel_id=1, source_target_pairs={{0,1},{1,2},{2,3},{3,0},{4,5},{5,6},{6,7},{7,4},{8,9},{9,10},{10,1... | collective-permute-start | bytes 3096584 | tf_op jit(solution)/shard_map/ppermute | solution.py:27
  40.8 3.1 %collective-permute-start.3 = (bf16[144,3584]{1,0:T(8,128)(2,1)S(1)}, bf16[144,3584]{1,0:T(8,128)(2,1)S(1)}, u32[]{:S(2)}, u32[]{:S(2)}) collective-permute-start(bf16[144,3584]{1,0:T(8,128)(2,1)S(1)} %slice.70), channel_id=1, source_target_pairs={{0,3},{1,0},{2,1},{3,2},{4,7},{5,4},{6,5},{7,6},{8,11},{9,8},{10,9... | collective-permute-start | bytes 3096584 | tf_op jit(solution)/shard_map/ppermute | solution.py:27
  44.0 3.4 %collective-permute-start.4 = (bf16[160,3584]{1,0:T(8,128)(2,1)}, bf16[160,3584]{1,0:T(8,128)(2,1)}, u32[]{:S(2)}, u32[]{:S(2)}) collective-permute-start(bf16[160,3584]{1,0:T(8,128)(2,1)} %pad.8), channel_id=1, source_target_pairs={{0,3},{1,0},{2,1},{3,2},{4,7},{5,4},{6,5},{7,6},{8,11},{9,8},{10,9... | collective-permute-start | bytes 3440648 | tf_op jit(solution)/shard_map/ppermute | solution.py:27
  47.4 1.9 %collective-permute-start.2 = (bf16[160,3584]{1,0:T(8,128)(2,1)}, bf16[160,3584]{1,0:T(8,128)(2,1)}, u32[]{:S(2)}, u32[]{:S(2)}) collective-permute-start(bf16[160,3584]{1,0:T(8,128)(2,1)} %pad.8), channel_id=1, source_target_pairs={{0,1},{1,2},{2,3},{3,0},{4,5},{5,6},{6,7},{7,4},{8,9},{9,10},{10,1... | collective-permute-start | bytes 3440648 | tf_op jit(solution)/shard_map/ppermute | solution.py:27
  49.3 12.4 %collective-permute-done.1.refs_1_ = bf16[144,3584]{1,0:T(8,128)(2,1)S(1)} collective-permute-done((bf16[144,3584]{1,0:T(8,128)(2,1)S(1)}, bf16[144,3584]{1,0:T(8,128)(2,1)S(1)}, u32[]{:S(2)}, u32[]{:S(2)}) %collective-permute-start.1) | collective-permute-done | bytes 1032224 | tf_op jit(solution)/shard_map/ppermute | solution.py:27
  61.7 9.9 %collective-permute-start.6 = (bf16[144,3584]{1,0:T(8,128)(2,1)S(1)}, bf16[144,3584]{1,0:T(8,128)(2,1)S(1)}, u32[]{:S(2)}, u32[]{:S(2)}) collective-permute-start(bf16[144,3584]{1,0:T(8,128)(2,1)S(1)} %collective-permute-done.1.refs_1_), channel_id=1, source_target_pairs={{0,4},{4,0},{1,5},{5,1},{2,6},{6,2},{3,7},{7,3},{8,12},{12,8},{9,1... | collective-permute-start | bytes 3096584 | tf_op jit(solution)/shard_map/ppermute | solution.py:27
  71.6 2.6 %collective-permute-start.8 = (bf16[144,3584]{1,0:T(8,128)(2,1)S(1)}, bf16[144,3584]{1,0:T(8,128)(2,1)S(1)}, u32[]{:S(2)}, u32[]{:S(2)}) collective-permute-start(bf16[144,3584]{1,0:T(8,128)(2,1)S(1)} %collective-permute-done.3.refs_3_), channel_id=1, source_target_pairs={{0,4},{4,0},{1,5},{5,1},{2,6},{6,2},{3,7},{7,3},{8,12},{12,8},{9,1... | collective-permute-start | bytes 3096584 | tf_op jit(solution)/shard_map/ppermute | solution.py:27
  77.0 11.0 %collective-permute-done.4.refs_4_ = bf16[160,3584]{1,0:T(8,128)(2,1)} collective-permute-done((bf16[160,3584]{1,0:T(8,128)(2,1)}, bf16[160,3584]{1,0:T(8,128)(2,1)}, u32[]{:S(2)}, u32[]{:S(2)}) %collective-permute-start.4) | collective-permute-done | bytes 1146912 | tf_op jit(solution)/shard_map/ppermute | solution.py:27
  88.0 4.5 %collective-permute-start.11 = (bf16[160,3584]{1,0:T(8,128)(2,1)}, bf16[160,3584]{1,0:T(8,128)(2,1)S(1)}, u32[]{:S(2)}, u32[]{:S(2)}) collective-permute-start(bf16[160,3584]{1,0:T(8,128)(2,1)} %collective-permute-done.4.refs_4_), channel_id=1, source_target_pairs={{0,3},{1,0},{2,1},{3,2},{4,7},{5,4},{6,5},{7,6},{8,11},{9,8},{10,9... | collective-permute-start | bytes 3440648 | tf_op jit(solution)/shard_map/ppermute | solution.py:27
  92.5 1.9 %collective-permute-start.10 = (bf16[144,3584]{1,0:T(8,128)(2,1)S(1)}, bf16[144,3584]{1,0:T(8,128)(2,1)}, u32[]{:S(2)}, u32[]{:S(2)}) collective-permute-start(bf16[144,3584]{1,0:T(8,128)(2,1)S(1)} %collective-permute-done.1.refs_1_), channel_id=1, source_target_pairs={{0,1},{1,2},{2,3},{3,0},{4,5},{5,6},{6,7},{7,4},{8,9},{9,10},{10,1... | collective-permute-start | bytes 3096584 | tf_op jit(solution)/shard_map/ppermute | solution.py:27
  96.4 6.7 %collective-permute-start.7 = (bf16[160,3584]{1,0:T(8,128)(2,1)}, bf16[160,3584]{1,0:T(8,128)(2,1)}, u32[]{:S(2)}, u32[]{:S(2)}) collective-permute-start(bf16[160,3584]{1,0:T(8,128)(2,1)} %collective-permute-done.2.refs_2_), channel_id=1, source_target_pairs={{0,4},{4,0},{1,5},{5,1},{2,6},{6,2},{3,7},{7,3},{8,12},{12,8},{9,1... | collective-permute-start | bytes 3440648 | tf_op jit(solution)/shard_map/ppermute | solution.py:27
  106.0 6.8 %collective-permute-done.11.refs_1_ = bf16[160,3584]{1,0:T(8,128)(2,1)S(1)} collective-permute-done((bf16[160,3584]{1,0:T(8,128)(2,1)}, bf16[160,3584]{1,0:T(8,128)(2,1)S(1)}, u32[]{:S(2)}, u32[]{:S(2)}) %collective-permute-start.11) | collective-permute-done | bytes 1146912 | tf_op jit(solution)/shard_map/ppermute | solution.py:27
  112.8 7.3 %collective-permute-start.13 = (bf16[160,3584]{1,0:T(8,128)(2,1)S(1)}, bf16[160,3584]{1,0:T(8,128)(2,1)}, u32[]{:S(2)}, u32[]{:S(2)}) collective-permute-start(bf16[160,3584]{1,0:T(8,128)(2,1)S(1)} %collective-permute-done.11.refs_1_), channel_id=1, source_target_pairs={{0,4},{4,0},{1,5},{5,1},{2,6},{6,2},{3,7},{7,3},{8,12},{12,8},{9,1... | collective-permute-start | bytes 3440648 | tf_op jit(solution)/shard_map/ppermute | solution.py:27
  120.1 2.7 %collective-permute-start.12 = (bf16[144,3584]{1,0:T(8,128)(2,1)}, bf16[144,3584]{1,0:T(8,128)(2,1)}, u32[]{:S(2)}, u32[]{:S(2)}) collective-permute-start(bf16[144,3584]{1,0:T(8,128)(2,1)} %collective-permute-done.10.refs_0_), channel_id=1, source_target_pairs={{0,4},{4,0},{1,5},{5,1},{2,6},{6,2},{3,7},{7,3},{8,12},{12,8},{9,1... | collective-permute-start | bytes 3096584 | tf_op jit(solution)/shard_map/ppermute | solution.py:27
  124.9 2.4 %shard_map.73 = (bf16[4,256,896]{2,1,0:T(8,128)(2,1)S(1)}, bf16[256,128]{1,0:T(8,128)(2,1)S(1)}) custom-call(bf16[1024,1024]{1,0:T(8,128)(2,1)} %bitcast.10.received), custom_call_target="tpu_custom_call" | custom-call | tf_op jit(solution)/shard_map/pallas_call | solution.py:65
  129.9 11.9 %shard_map.74.carried = f32[8,256]{1,0:T(8,128)S(1)} custom-call(s32[6]{0:T(128)S(1)} %stack.69.starts, bf16[4,256,896]{2,1,0:T(8,128)(2,1)S(1)} %get-tuple-element.11.tokens, bf16[256,128]{1,0:T(8,128)(2,1)S(1)} %get-tuple-element.12.notes, f32[8,256]{1,0:T(8,128)S(1)} %copy-done.9, bf16[297,3584]{1,0:T(8,128)(2,1)S(1)} %copy-done, ...), custom_call_target="tpu_custom_call" | custom-call | flops 3321364480 | bytes 12974080 | tf_op jit(solution)/shard_map/pallas_call | solution.py:139
  141.7 2.2 %shard_map.75.carried = f32[8,256]{1,0:T(8,128)S(1)} custom-call(s32[1]{0:T(128)} %bitcast.11.starts, bf16[4,256,896]{2,1,0:T(8,128)(2,1)S(1)} %get-tuple-element.11.tokens, bf16[256,128]{1,0:T(8,128)(2,1)S(1)} %get-tuple-element.12.notes, f32[8,256]{1,0:T(8,128)S(1)} %shard_map.74.carried, bf16[144,3584]{1,0:T(8,128)(2,1)} %collective-permute-done.10.refs_0_, ...), custom_call_target="tpu_custom_call" | custom-call | flops 557842432 | bytes 2179072 | tf_op jit(solution)/shard_map/pallas_call | solution.py:139
  143.9 2.5 %shard_map.76 = f32[8,256]{1,0:T(8,128)S(1)} custom-call(s32[1]{0:T(128)} %bitcast.9.starts, bf16[4,256,896]{2,1,0:T(8,128)(2,1)S(1)} %get-tuple-element.11.tokens, bf16[256,128]{1,0:T(8,128)(2,1)S(1)} %get-tuple-element.12.notes, f32[8,256]{1,0:T(8,128)S(1)} %shard_map.75.carried, bf16[144,3584]{1,0:T(8,128)(2,1)} %collective-permute-done.12.refs_0_, ...), custom_call_target="tpu_custom_call" | custom-call | flops 557842432 | bytes 2179072 | tf_op jit(solution)/shard_map/pallas_call | solution.py:139
  147.5 17.7 %all-to-all-start.2 = ((f32[256,1,16]{2,1,0:T(1,128)}), f32[256,1,16]{2,1,0:T(1,128)S(1)}, u32[]{:S(2)}, u32[]{:S(2)}) async-start(f32[256,1,16]{2,1,0:T(1,128)} %bitcast.20), calls=%async_computation.2 | async-start | bytes 262144 | tf_op jit(solution)/shard_map/all_to_all | solution.py:36
  165.8 11.3 %all-to-all-done.2 = f32[256,1,16]{2,1,0:T(1,128)S(1)} async-done(((f32[256,1,16]{2,1,0:T(1,128)}), f32[256,1,16]{2,1,0:T(1,128)S(1)}, u32[]{:S(2)}, u32[]{:S(2)}) %all-to-all-start.2) | async-done | bytes 16416 | tf_op jit(solution)/shard_map/all_to_all | solution.py:36
  (82 shorter events, 24.9 us)
Async XLA Ops:
  4.1 10.3 %all-to-all-start = ((bf16[4,8,896]{2,1,0:T(8,128)(2,1)}), bf16[4,8,896]{2,1,0:T(8,128)(2,1)S(1)}, u32[]{:S(2)}, u32[]{:S(2)}) async-start(bf16[4,8,896]{2,1,0:T(8,128)(2,1)} %pad_maximum_fusion), calls=%async_computation | async-start | bytes 114688 | tf_op jit(solution)/shard_map/all_to_all | solution.py:36
  12.0 1.3 slice-start
  14.6 7.4 %collective-permute-start = (bf16[4,4,1024]{2,1,0:T(4,128)(2,1)S(1)}, bf16[4,4,1024]{2,1,0:T(4,128)(2,1)S(1)}, u32[]{:S(2)}, u32[]{:S(2)}) collective-permute-start(bf16[4,4,1024]{2,1,0:T(4,128)(2,1)S(1)} %slice.89), channel_id=1, source_target_pairs={{0,4},{4,8},{8,12},{12,16},{16,20},{20,24},{24,28},{28,32},{32,36}... | collective-permute-start | bytes 98312 | tf_op jit(solution)/shard_map/ppermute | solution.py:32
  23.7 51.4 %copy-start = (bf16[297,3584]{1,0:T(8,128)(2,1)S(1)}, bf16[297,3584]{1,0:T(8,128)(2,1)}, u32[]{:S(2)}) copy-start(bf16[297,3584]{1,0:T(8,128)(2,1)} %refs_0_.1) | copy-start | bytes 6386692
  23.7 101.1 %copy-start.11 = (s32[4]{0:T(128)S(1)}, s32[4]{0:T(128)}, u32[]{:S(2)}) copy-start(s32[4]{0:T(128)} %param.12) | copy-start | bytes 52
  23.7 101.2 %all-to-all-start.1 = ((bf16[64,16,1024]{2,1,0:T(8,128)(2,1)}), bf16[64,16,1024]{2,1,0:T(8,128)(2,1)}, u32[]{:S(2)}, u32[]{:S(2)}) async-start(bf16[64,16,1024]{2,1,0:T(8,128)(2,1)} %broadcast_in_dim.12), calls=%async_computation.1 | async-start | bytes 4194304 | tf_op jit(solution)/shard_map/all_to_all | solution.py:36
  37.3 90.1 %copy-start.9 = (f32[8,256]{1,0:T(8,128)S(1)}, f32[8,256]{1,0:T(8,128)}, u32[]{:S(2)}) copy-start(f32[8,256]{1,0:T(8,128)} %constant.131.clone.1.carried) | copy-start | bytes 24580
  37.3 24.3 %collective-permute-start.1 = (bf16[144,3584]{1,0:T(8,128)(2,1)S(1)}, bf16[144,3584]{1,0:T(8,128)(2,1)S(1)}, u32[]{:S(2)}, u32[]{:S(2)}) collective-permute-start(bf16[144,3584]{1,0:T(8,128)(2,1)S(1)} %slice.70), channel_id=1, source_target_pairs={{0,1},{1,2},{2,3},{3,0},{4,5},{5,6},{6,7},{7,4},{8,9},{9,10},{10,1... | collective-permute-start | bytes 3096584 | tf_op jit(solution)/shard_map/ppermute | solution.py:27
  40.8 30.7 %collective-permute-start.3 = (bf16[144,3584]{1,0:T(8,128)(2,1)S(1)}, bf16[144,3584]{1,0:T(8,128)(2,1)S(1)}, u32[]{:S(2)}, u32[]{:S(2)}) collective-permute-start(bf16[144,3584]{1,0:T(8,128)(2,1)S(1)} %slice.70), channel_id=1, source_target_pairs={{0,3},{1,0},{2,1},{3,2},{4,7},{5,4},{6,5},{7,6},{8,11},{9,8},{10,9... | collective-permute-start | bytes 3096584 | tf_op jit(solution)/shard_map/ppermute | solution.py:27
  44.0 44.0 %collective-permute-start.4 = (bf16[160,3584]{1,0:T(8,128)(2,1)}, bf16[160,3584]{1,0:T(8,128)(2,1)}, u32[]{:S(2)}, u32[]{:S(2)}) collective-permute-start(bf16[160,3584]{1,0:T(8,128)(2,1)} %pad.8), channel_id=1, source_target_pairs={{0,3},{1,0},{2,1},{3,2},{4,7},{5,4},{6,5},{7,6},{8,11},{9,8},{10,9... | collective-permute-start | bytes 3440648 | tf_op jit(solution)/shard_map/ppermute | solution.py:27
  47.4 45.1 %collective-permute-start.2 = (bf16[160,3584]{1,0:T(8,128)(2,1)}, bf16[160,3584]{1,0:T(8,128)(2,1)}, u32[]{:S(2)}, u32[]{:S(2)}) collective-permute-start(bf16[160,3584]{1,0:T(8,128)(2,1)} %pad.8), channel_id=1, source_target_pairs={{0,1},{1,2},{2,3},{3,0},{4,5},{5,6},{6,7},{7,4},{8,9},{9,10},{10,1... | collective-permute-start | bytes 3440648 | tf_op jit(solution)/shard_map/ppermute | solution.py:27
  61.7 33.7 %collective-permute-start.6 = (bf16[144,3584]{1,0:T(8,128)(2,1)S(1)}, bf16[144,3584]{1,0:T(8,128)(2,1)S(1)}, u32[]{:S(2)}, u32[]{:S(2)}) collective-permute-start(bf16[144,3584]{1,0:T(8,128)(2,1)S(1)} %collective-permute-done.1.refs_1_), channel_id=1, source_target_pairs={{0,4},{4,0},{1,5},{5,1},{2,6},{6,2},{3,7},{7,3},{8,12},{12,8},{9,1... | collective-permute-start | bytes 3096584 | tf_op jit(solution)/shard_map/ppermute | solution.py:27
  71.6 31.5 %collective-permute-start.8 = (bf16[144,3584]{1,0:T(8,128)(2,1)S(1)}, bf16[144,3584]{1,0:T(8,128)(2,1)S(1)}, u32[]{:S(2)}, u32[]{:S(2)}) collective-permute-start(bf16[144,3584]{1,0:T(8,128)(2,1)S(1)} %collective-permute-done.3.refs_3_), channel_id=1, source_target_pairs={{0,4},{4,0},{1,5},{5,1},{2,6},{6,2},{3,7},{7,3},{8,12},{12,8},{9,1... | collective-permute-start | bytes 3096584 | tf_op jit(solution)/shard_map/ppermute | solution.py:27
  75.1 52.3 %collective-permute-start.5 = (bf16[297,3584]{1,0:T(8,128)(2,1)S(1)}, bf16[297,3584]{1,0:T(8,128)(2,1)}, u32[]{:S(2)}, u32[]{:S(2)}) collective-permute-start(bf16[297,3584]{1,0:T(8,128)(2,1)S(1)} %copy-done), channel_id=1, source_target_pairs={{0,4},{4,0},{1,5},{5,1},{2,6},{6,2},{3,7},{7,3},{8,12},{12,8},{9,1... | collective-permute-start | bytes 6386696 | tf_op jit(solution)/shard_map/ppermute | solution.py:27
  88.0 24.9 %collective-permute-start.11 = (bf16[160,3584]{1,0:T(8,128)(2,1)}, bf16[160,3584]{1,0:T(8,128)(2,1)S(1)}, u32[]{:S(2)}, u32[]{:S(2)}) collective-permute-start(bf16[160,3584]{1,0:T(8,128)(2,1)} %collective-permute-done.4.refs_4_), channel_id=1, source_target_pairs={{0,3},{1,0},{2,1},{3,2},{4,7},{5,4},{6,5},{7,6},{8,11},{9,8},{10,9... | collective-permute-start | bytes 3440648 | tf_op jit(solution)/shard_map/ppermute | solution.py:27
  92.5 27.7 %collective-permute-start.10 = (bf16[144,3584]{1,0:T(8,128)(2,1)S(1)}, bf16[144,3584]{1,0:T(8,128)(2,1)}, u32[]{:S(2)}, u32[]{:S(2)}) collective-permute-start(bf16[144,3584]{1,0:T(8,128)(2,1)S(1)} %collective-permute-done.1.refs_1_), channel_id=1, source_target_pairs={{0,1},{1,2},{2,3},{3,0},{4,5},{5,6},{6,7},{7,4},{8,9},{9,10},{10,1... | collective-permute-start | bytes 3096584 | tf_op jit(solution)/shard_map/ppermute | solution.py:27
  96.4 31.0 %collective-permute-start.7 = (bf16[160,3584]{1,0:T(8,128)(2,1)}, bf16[160,3584]{1,0:T(8,128)(2,1)}, u32[]{:S(2)}, u32[]{:S(2)}) collective-permute-start(bf16[160,3584]{1,0:T(8,128)(2,1)} %collective-permute-done.2.refs_2_), channel_id=1, source_target_pairs={{0,4},{4,0},{1,5},{5,1},{2,6},{6,2},{3,7},{7,3},{8,12},{12,8},{9,1... | collective-permute-start | bytes 3440648 | tf_op jit(solution)/shard_map/ppermute | solution.py:27
  104.1 23.3 %collective-permute-start.9 = (bf16[160,3584]{1,0:T(8,128)(2,1)}, bf16[160,3584]{1,0:T(8,128)(2,1)}, u32[]{:S(2)}, u32[]{:S(2)}) collective-permute-start(bf16[160,3584]{1,0:T(8,128)(2,1)} %collective-permute-done.4.refs_4_), channel_id=1, source_target_pairs={{0,4},{4,0},{1,5},{5,1},{2,6},{6,2},{3,7},{7,3},{8,12},{12,8},{9,1... | collective-permute-start | bytes 3440648 | tf_op jit(solution)/shard_map/ppermute | solution.py:27
  112.8 31.1 %collective-permute-start.13 = (bf16[160,3584]{1,0:T(8,128)(2,1)S(1)}, bf16[160,3584]{1,0:T(8,128)(2,1)}, u32[]{:S(2)}, u32[]{:S(2)}) collective-permute-start(bf16[160,3584]{1,0:T(8,128)(2,1)S(1)} %collective-permute-done.11.refs_1_), channel_id=1, source_target_pairs={{0,4},{4,0},{1,5},{5,1},{2,6},{6,2},{3,7},{7,3},{8,12},{12,8},{9,1... | collective-permute-start | bytes 3440648 | tf_op jit(solution)/shard_map/ppermute | solution.py:27
  120.1 23.8 %collective-permute-start.12 = (bf16[144,3584]{1,0:T(8,128)(2,1)}, bf16[144,3584]{1,0:T(8,128)(2,1)}, u32[]{:S(2)}, u32[]{:S(2)}) collective-permute-start(bf16[144,3584]{1,0:T(8,128)(2,1)} %collective-permute-done.10.refs_0_), channel_id=1, source_target_pairs={{0,4},{4,0},{1,5},{5,1},{2,6},{6,2},{3,7},{7,3},{8,12},{12,8},{9,1... | collective-permute-start | bytes 3096584 | tf_op jit(solution)/shard_map/ppermute | solution.py:27
  124.9 2.5 %copy-start.2 = (bf16[144,3584]{1,0:T(8,128)(2,1)S(1)}, bf16[144,3584]{1,0:T(8,128)(2,1)}, u32[]{:S(2)}) copy-start(bf16[144,3584]{1,0:T(8,128)(2,1)} %copy-done.1) | copy-start | bytes 3096580
  124.9 2.5 %copy-start.4 = (bf16[144,3584]{1,0:T(8,128)(2,1)S(1)}, bf16[144,3584]{1,0:T(8,128)(2,1)}, u32[]{:S(2)}) copy-start(bf16[144,3584]{1,0:T(8,128)(2,1)} %copy-done.3) | copy-start | bytes 3096580
  127.4 1.2 copy-start.6
  147.5 29.7 %all-to-all-start.2 = ((f32[256,1,16]{2,1,0:T(1,128)}), f32[256,1,16]{2,1,0:T(1,128)S(1)}, u32[]{:S(2)}, u32[]{:S(2)}) async-start(f32[256,1,16]{2,1,0:T(1,128)} %bitcast.20), calls=%async_computation.2 | async-start | bytes 262144 | tf_op jit(solution)/shard_map/all_to_all | solution.py:36
  (6 other events, 5.9 us)

commit v3 on v2

v3 whole, which is shorter than its diff:
```python
import functools

import jax
import jax.numpy as jnp
from jax import lax
from jax.experimental import pallas as pl
from jax.experimental.pallas import tpu as pltpu
from jax.sharding import Mesh
from jax.sharding import PartitionSpec as P


BLK_DEV = 2
DP = ("dp_0", "dp_1", "dp_2")
PLANE = ("dp_0", "dp_1")
DP_TENSOR = ("dp_0", "dp_1", "dp_2", "tensor")

GRID = (8, 8)
INTERPRET = False
epsilon = 1e-06
NOTES = 128
STATS = 4
VMEM_LIMIT = 32 * 1024 * 1024
AHEAD = 2


def around(block, axis, step):
    size = lax.axis_size(axis)
    return lax.ppermute(block, axis, [(i, (i + step) % size) for i in range(size)])


def from_behind(block):
    devices = lax.axis_size(DP)
    return lax.ppermute(block, DP, [(i, i + 1) for i in range(devices - 1)])


def exchange(pieces, axes):
    return lax.all_to_all(pieces, axes, split_axis=0, concat_axis=0, tiled=True)


def to_everyone(shard, axes):
    return exchange(jnp.broadcast_to(shard[None], (lax.axis_size(axes), *shard.shape)), axes)


def arrange(received, tokens, notes, per_source):
    ways, _, width = tokens.shape
    group = min(256, received.shape[0])
    share = group // ways
    row = lax.broadcasted_iota(jnp.int32, (group, group), 0)
    column = lax.broadcasted_iota(jnp.int32, (group, group), 1)
    token = row % share
    wanted = token // per_source * (ways * per_source) + token % per_source
    wanted = wanted + row // share * per_source
    pick = jnp.where(column == wanted, 1.0, 0.0).astype(jnp.bfloat16)
    for block in range(received.shape[0] // group):
        rows = received[block * group : (block + 1) * group, :]
        placed = jnp.dot(pick, rows, preferred_element_type=jnp.float32).astype(jnp.bfloat16)
        here = slice(block * share, (block + 1) * share)
        for q in range(ways):
            tokens[q, here, :] = placed[q * share : (q + 1) * share, :width]
        notes[here, :] = placed[:share, width:]


def absorb(copies, held, starts, tokens, notes, carried, stats):
    quarters, _, width = tokens.shape
    lane = lax.broadcasted_iota(jnp.int32, (8, NOTES), 1)
    powers = jnp.where(lane == 0, 1.0, jnp.where(lane == 1, 256.0, 65536.0))
    powers = jnp.where(lane < 3, powers, 0.0).astype(jnp.bfloat16)
    labels = lax.dot_general(
        powers, notes[...], (((1,), (1,)), ((), ())), preferred_element_type=jnp.float32
    )[0:1].astype(jnp.int32)
    peak, exp_sum, square_sum, label_logit = (carried[i : i + 1, :] for i in range(STATS))
    for index, chunk in enumerate(held):
        copies[index].wait()
        if index + AHEAD < len(copies):
            copies[index + AHEAD].start()
        logits = sum(
            lax.dot_general(
                chunk[:, q * width : (q + 1) * width],
                tokens[q],
                (((1,), (1,)), ((), ())),
                preferred_element_type=jnp.float32,
            )
            for q in range(quarters)
        )
        ids = lax.broadcasted_iota(jnp.int32, logits.shape, 0)
        new_peak = jnp.maximum(peak, jnp.max(logits, axis=0, keepdims=True))
        rescale = jnp.exp(peak - new_peak)
        scaled = jnp.exp(logits - new_peak)
        hit = ids == labels - starts[index]
        exp_sum = exp_sum * rescale + jnp.sum(scaled, axis=0, keepdims=True)
        square_sum = square_sum * (rescale * rescale) + jnp.sum(
            scaled * scaled, axis=0, keepdims=True
        )
        label_logit = label_logit + jnp.sum(jnp.where(hit, logits, 0.0), axis=0, keepdims=True)
        peak = new_peak
    stats[0:1, :] = peak
    stats[1:2, :] = exp_sum
    stats[2:3, :] = square_sum
    stats[3:4, :] = label_logit
    stats[4:8, :] = jnp.zeros((4, stats.shape[1]), jnp.float32)


def copies_of(sources, held, arrival):
    copies = [
        pltpu.make_async_copy(source, target, arrival.at[index])
        for index, (source, target) in enumerate(zip(sources, held))
    ]
    for copy in copies[:AHEAD]:
        copy.start()
    return copies


def first_body(count, per_source, starts, received, carried, *refs):
    sources, (stats, tokens, notes) = refs[:count], refs[count : count + 3]
    held, arrival = refs[count + 3 : -1], refs[-1]
    copies = copies_of(sources, held, arrival)
    arrange(received, tokens, notes, per_source)
    absorb(copies, held, starts, tokens, notes, carried, stats)


def next_body(count, starts, tokens, notes, carried, *refs):
    sources, stats, held, arrival = refs[:count], refs[count], refs[count + 1 : -1], refs[-1]
    copies = copies_of(sources, held, arrival)
    absorb(copies, held, starts, tokens, notes, carried, stats)


def absorbed(body, inputs, chunks, count, outputs):
    starts = jnp.stack([start for _, start in chunks])
    arrays = [chunk for chunk, _ in chunks]
    rows, depth = sum(chunk.shape[0] for chunk in arrays), arrays[0].shape[1]
    vmem = pl.BlockSpec(memory_space=pltpu.VMEM)
    return pl.pallas_call(
        body,
        out_shape=outputs,
        in_specs=[pl.BlockSpec(memory_space=pltpu.SMEM)]
        + [vmem] * len(inputs)
        + [pl.BlockSpec(memory_space=pl.ANY if INTERPRET else pltpu.HBM)] * len(arrays),
        out_specs=[vmem] * len(outputs),
        scratch_shapes=[pltpu.VMEM(chunk.shape, chunk.dtype) for chunk in arrays]
        + [pltpu.SemaphoreType.DMA((len(arrays),))],
        interpret=INTERPRET,
        cost_estimate=pl.CostEstimate(
            flops=2 * rows * count * depth,
            bytes_accessed=2 * rows * depth,
            transcendentals=rows * count,
        ),
        compiler_params=pltpu.CompilerParams(vmem_limit_bytes=VMEM_LIMIT),
    )(starts, *inputs, *arrays)


def per_device(hidden, norm_gain, head_weight, counts, destination, lengths, labels):
    capacity, block_len, width = hidden.shape
    ways = lax.axis_size("tensor")
    tall, wide = lax.axis_size("dp_0"), lax.axis_size("dp_1")
    plane = tall * wide
    dp_index = lax.axis_index(DP)
    core_index = lax.axis_index("dp_2")
    tensor_index = lax.axis_index("tensor")
    share = BLK_DEV * block_len // ways
    cuts = block_len // share
    row_width = width + NOTES

    sliced = jnp.moveaxis(hidden.reshape(capacity, cuts, share, width), 1, 0)
    sliced = sliced.reshape(cuts, capacity * share, width)
    gathered = exchange(jnp.tile(sliced, (ways // cuts, 1, 1)), "tensor")

    vocab_rows = head_weight.shape[0]
    half = vocab_rows // 2 // 16 * 16
    weight, gathered, counts, destination, labels, lengths = lax.optimization_barrier(
        (head_weight, gathered, counts, destination, labels, lengths)
    )
    low = around(weight, "tensor", 1)
    high = around(weight, "tensor", -1)

    values = gathered.astype(jnp.float32)
    mean_square = jnp.sum(values * values, axis=(0, 2), keepdims=True) / (ways * width)
    gain = norm_gain.reshape(ways, 1, width)
    normed = (values * lax.rsqrt(mean_square + epsilon) * gain).astype(jnp.bfloat16)
    normed = normed.reshape(ways, capacity, share, width)

    is_live = jnp.arange(capacity, dtype=jnp.int32) < counts[0]
    stay = jnp.sum(is_live & (destination == dp_index)).astype(jnp.int32)
    short = stay < BLK_DEV
    first = tensor_index < cuts
    from_first = first | short

    facts = jnp.stack(
        [labels % 256, labels // 256 % 256, labels // 65536]
        + [jnp.broadcast_to(lengths[:, None], labels.shape)],
        axis=-1,
    ).astype(jnp.float32)
    facts = facts.reshape(capacity, cuts, share, 4)
    facts = jnp.where(tensor_index % cuts == 0, facts[:, 0], facts[:, 1]).astype(jnp.bfloat16)

    def with_facts(near_slot, far_slot, nearer):
        rows = jnp.where(nearer, normed[:, near_slot], normed[:, far_slot])
        notes = jnp.where(nearer, facts[near_slot], facts[far_slot])
        notes = jnp.pad(notes[None], ((0, ways - 1), (0, 0), (0, NOTES - 4)))
        return jnp.concatenate([rows, notes], axis=2)

    own = with_facts(0, 1, from_first)
    arrived = from_behind(with_facts(1, 2, short))
    message = jnp.where(short & first, arrived, own)
    arrived_length = arrived[0, 0, width + 3].astype(jnp.int32)
    local_lengths = jnp.where(
        short, jnp.stack([arrived_length, lengths[0]]), jnp.stack([lengths[0], lengths[1]])
    )

    received = to_everyone(message.reshape(ways * share, row_width), PLANE)
    far_low = around(low[:half], "tensor", 1)
    far_high = around(high[half:], "tensor", -1)

    partner = 1 - core_index
    chip = (lax.axis_index("dp_0") * wide + lax.axis_index("dp_1")) * 2

    def start_of(core, step, row=0):
        return ((chip + core) * ways + (tensor_index + step) % ways) * vocab_rows + row

    held = ((weight, 0, 0), (low, -1, 0), (high, 1, 0))
    far = ((far_low, 2, 0), (far_high, 2, half))

    def chunks_of(core, pieces):
        return [(piece, start_of(core, step, row)) for piece, step, row in pieces]

    def crossed(pieces):
        return [(around(piece, "dp_2", 1), step, row) for piece, step, row in pieces]

    count = plane * share
    received = received.reshape(count * ways, row_width)
    empty = jnp.concatenate(
        [jnp.full((1, count), -jnp.inf, jnp.float32), jnp.zeros((7, count), jnp.float32)]
    )
    results = [jax.ShapeDtypeStruct((8, count), jnp.float32)]
    arranged = [
        jax.ShapeDtypeStruct((ways, count, width), jnp.bfloat16),
        jax.ShapeDtypeStruct((count, NOTES), jnp.bfloat16),
    ]
    near = chunks_of(core_index, held) + chunks_of(partner, crossed(held))
    body = functools.partial(first_body, len(near), share)
    outputs = results + arranged
    stats, tokens, notes = absorbed(body, (received, empty), near, count, outputs)
    body = functools.partial(next_body, len(far))
    for core, pieces in ((core_index, far), (partner, crossed(far))):
        (stats,) = absorbed(body, (tokens, notes, stats), chunks_of(core, pieces), count, results)

    stats = stats[:STATS].reshape(STATS, plane, share)
    sums = exchange(jnp.moveaxis(stats, 1, 0).reshape(plane, STATS * share), PLANE)
    part_peak = sums[:, :share]
    peak = jnp.max(part_peak, axis=0)
    rescale = jnp.exp(part_peak - peak[None])
    exp_sum = jnp.sum(sums[:, share : 2 * share] * rescale, axis=0)
    square_sum = jnp.sum(sums[:, 2 * share : 3 * share] * rescale * rescale, axis=0)
    label_logit = jnp.sum(sums[:, 3 * share :], axis=0)
    share_error = (
        square_sum / (exp_sum * exp_sum) - 2.0 * jnp.exp(label_logit - peak) / exp_sum + 1.0
    )
    token_error = to_everyone(share_error, "tensor").reshape(BLK_DEV, block_len)
    valid = jnp.arange(block_len, dtype=jnp.int32)[None, :] < local_lengths[:, None]
    return jnp.sum(jnp.where(valid, token_error, 0.0), axis=1) / local_lengths.astype(jnp.float32)


def solution(mesh):
    dp, tensor = mesh.shape["dp"], mesh.shape["tensor"]
    finer = Mesh(mesh.devices.reshape(*GRID, dp // (GRID[0] * GRID[1]), tensor), DP_TENSOR)
    placed = (P(DP, None, "tensor"), P(), P(DP_TENSOR, None), P(DP), P(DP), P(DP), P(DP, None))
    return jax.shard_map(per_device, mesh=finer, in_specs=placed, out_specs=P(DP), check_vma=False)
```

time: 180 us -> 174 us (0.967)
  starting transfers between devices: 91.5 us -> 69.3 us
  waiting for transfers between devices: 44.7 us -> 60.1 us
  blocking collectives: 0 us -> 6.47 us
  local copies, waits for them, and re-layouts: 14.9 us -> 11.3 us
  other arithmetic: 6.18 us -> 3.71 us
    ppermute x13 -> x9, starting transfers between devices: 51.2 us -> 28.5 us  [around(): lax.ppermute(block, axis, [(i, (i + step) % size) for i in range(size)])]
    ppermute x13 -> x9, waiting for transfers between devices: 30.2 us -> 46.2 us  [around(): lax.ppermute(block, axis, [(i, (i + step) % size) for i in range(size)])]
    all_to_all x0 -> x1, blocking collectives: none -> 6.47 us  [exchange(): return lax.all_to_all(pieces, axes, split_axis=0, concat_axis=0, tiled=True)]
    unnamed x25 -> x6, local copies, waits for them, and re-layouts: 7.06 us -> 1.62 us
    ppermute x1, waiting for transfers between devices: 3.17 us -> 0.01 us  [from_behind(): return lax.ppermute(block, DP, [(i, i + 1) for i in range(devices - 1)])]
    all_to_all x3, waiting for transfers between devices: 11.4 us -> 13.9 us  [exchange(): return lax.all_to_all(pieces, axes, split_axis=0, concat_axis=0, tiled=True)]
    pallas_call x4 -> x3, Pallas kernels: 19 us -> 19.4 us  [absorbed(): pl.pallas_call(body, out_shape=outputs, in_specs=[pl.BlockSpec(memory_spa...]
  transfers between devices with their start and end apart: 17 -> 13, of which waited for: 5 -> 5; matrix products, arithmetic and copies ran while one was open for 3% -> 4% of each run, Pallas kernels for 9% -> 9%
where the time goes in v3:
time: 174 us; the launch traced here: 173 us
  starting transfers between devices  69.3 us (40%)
  waiting for transfers between devices  60.1 us (35%)
  Pallas kernels  19.4 us (11%)
  local copies, waits for them, and re-layouts  11.3 us (6%)
  blocking collectives  6.47 us (4%)
  other arithmetic  3.71 us (2%)
  between operations  2.3 us (1%)
    ppermute x9, waiting for transfers between devices, around(): lax.ppermute(block, axis, [(i, (i + step) % size) for i in range(size)])  46.2 us
    all_to_all x3, starting transfers between devices, exchange(): return lax.all_to_all(pieces, axes, split_axis=0, concat_axis=0, tiled=True)  35.6 us
    ppermute x9, starting transfers between devices, around(): lax.ppermute(block, axis, [(i, (i + step) % size) for i in range(size)])  28.5 us
    pallas_call x3, Pallas kernels, absorbed(): pl.pallas_call(body, out_shape=outputs, in_specs=[pl.BlockSpec(memory_spa...  19.4 us
    all_to_all x3, waiting for transfers between devices, exchange(): return lax.all_to_all(pieces, axes, split_axis=0, concat_axis=0, tiled=True)  13.9 us
    all_to_all x1, blocking collectives, exchange(): return lax.all_to_all(pieces, axes, split_axis=0, concat_axis=0, tiled=True)  6.47 us
    ppermute x1, starting transfers between devices, from_behind(): return lax.ppermute(block, DP, [(i, i + 1) for i in range(devices - 1)])  5.19 us
  transfers between devices with their start and end apart: 13, of which 5 were waited for; matrix products, arithmetic and copies ran while one was open for 4% of the time, Pallas kernels for 9%

profile of v3, /device:TPU:1, one launch (start us, length us, event | category | flops | bytes accessed | tf_op | source)
XLA Modules:
  0.0 172.6 jit_solution(17427101282336916295)
XLA Ops:
  1.6 4.8 %all-to-all-start = ((bf16[4,16,896]{2,1,0:T(8,128)(2,1)}), bf16[4,16,896]{2,1,0:T(8,128)(2,1)S(1)}, u32[]{:S(2)}, u32[]{:S(2)}) async-start(bf16[4,16,896]{2,1,0:T(8,128)(2,1)} %bitcast.3), calls=%async_computation | async-start | bytes 229376 | tf_op jit(solution)/shard_map/all_to_all | solution.py:37
  7.8 3.4 %all-to-all-done = bf16[4,16,896]{2,1,0:T(8,128)(2,1)S(1)} async-done(((bf16[4,16,896]{2,1,0:T(8,128)(2,1)}), bf16[4,16,896]{2,1,0:T(8,128)(2,1)S(1)}, u32[]{:S(2)}, u32[]{:S(2)}) %all-to-all-start) | async-done | bytes 114720 | tf_op jit(solution)/shard_map/all_to_all | solution.py:37
  15.2 5.2 %collective-permute-start = (bf16[4,4,1024]{2,0,1:T(4,128)(2,1)S(1)}, bf16[4,4,1024]{2,0,1:T(4,128)(2,1)S(1)}, u32[]{:S(2)}, u32[]{:S(2)}) collective-permute-start(bf16[4,4,1024]{2,0,1:T(4,128)(2,1)S(1)} %fusion.6), channel_id=1, source_target_pairs={{0,4},{4,8},{8,12},{12,16},{16,20},{20,24},{24,28},{28,32},{32,36}... | collective-permute-start | bytes 98312 | tf_op jit(solution)/shard_map/ppermute | solution.py:33
  20.4 2.2 %collective-permute-start.1 = (bf16[297,3584]{1,0:T(8,128)(2,1)}, bf16[297,3584]{1,0:T(8,128)(2,1)}, u32[]{:S(2)}, u32[]{:S(2)}) collective-permute-start(bf16[297,3584]{1,0:T(8,128)(2,1)} %refs_0_), channel_id=1, source_target_pairs={{0,1},{1,2},{2,3},{3,0},{4,5},{5,6},{6,7},{7,4},{8,9},{9,10},{10,1... | collective-permute-start | bytes 6386696 | tf_op jit(solution)/shard_map/ppermute | solution.py:28
  22.6 4.3 %collective-permute-start.2 = (bf16[297,3584]{1,0:T(8,128)(2,1)}, bf16[297,3584]{1,0:T(8,128)(2,1)}, u32[]{:S(2)}, u32[]{:S(2)}) collective-permute-start(bf16[297,3584]{1,0:T(8,128)(2,1)} %refs_0_), channel_id=1, source_target_pairs={{0,3},{1,0},{2,1},{3,2},{4,7},{5,4},{6,5},{7,6},{8,11},{9,8},{10,9... | collective-permute-start | bytes 6386696 | tf_op jit(solution)/shard_map/ppermute | solution.py:28
  27.1 1.6 broadcast_in_dim.10
  28.7 15.4 %all-to-all-start.1 = ((bf16[64,16,1024]{2,1,0:T(8,128)(2,1)}), bf16[64,16,1024]{2,1,0:T(8,128)(2,1)S(1)}, u32[]{:S(2)}, u32[]{:S(2)}) async-start(bf16[64,16,1024]{2,1,0:T(8,128)(2,1)} %broadcast_in_dim.10), calls=%async_computation.1 | async-start | bytes 4194304 | tf_op jit(solution)/shard_map/all_to_all | solution.py:37
  44.2 2.5 %collective-permute-start.3 = (bf16[297,3584]{1,0:T(8,128)(2,1)}, bf16[297,3584]{1,0:T(8,128)(2,1)}, u32[]{:S(2)}, u32[]{:S(2)}) collective-permute-start(bf16[297,3584]{1,0:T(8,128)(2,1)} %refs_0_), channel_id=1, source_target_pairs={{0,4},{4,0},{1,5},{5,1},{2,6},{6,2},{3,7},{7,3},{8,12},{12,8},{9,1... | collective-permute-start | bytes 6386696 | tf_op jit(solution)/shard_map/ppermute | solution.py:28
  46.7 23.6 %collective-permute-done.1.refs_1_ = bf16[297,3584]{1,0:T(8,128)(2,1)} collective-permute-done((bf16[297,3584]{1,0:T(8,128)(2,1)}, bf16[297,3584]{1,0:T(8,128)(2,1)}, u32[]{:S(2)}, u32[]{:S(2)}) %collective-permute-start.1) | collective-permute-done | bytes 2128928 | tf_op jit(solution)/shard_map/ppermute | solution.py:28
  70.3 5.3 %collective-permute-start.4 = (bf16[297,3584]{1,0:T(8,128)(2,1)}, bf16[297,3584]{1,0:T(8,128)(2,1)}, u32[]{:S(2)}, u32[]{:S(2)}) collective-permute-start(bf16[297,3584]{1,0:T(8,128)(2,1)} %collective-permute-done.1.refs_1_), channel_id=1, source_target_pairs={{0,4},{4,0},{1,5},{5,1},{2,6},{6,2},{3,7},{7,3},{8,12},{12,8},{9,1... | collective-permute-start | bytes 6386696 | tf_op jit(solution)/shard_map/ppermute | solution.py:28
  75.6 1.9 %collective-permute-start.5 = (bf16[297,3584]{1,0:T(8,128)(2,1)}, bf16[297,3584]{1,0:T(8,128)(2,1)}, u32[]{:S(2)}, u32[]{:S(2)}) collective-permute-start(bf16[297,3584]{1,0:T(8,128)(2,1)} %collective-permute-done.2.refs_2_), channel_id=1, source_target_pairs={{0,4},{4,0},{1,5},{5,1},{2,6},{6,2},{3,7},{7,3},{8,12},{12,8},{9,1... | collective-permute-start | bytes 6386696 | tf_op jit(solution)/shard_map/ppermute | solution.py:28
  77.5 1.3 slice.86
  78.8 4.6 %collective-permute-start.7 = (bf16[153,3584]{1,0:T(8,128)(2,1)S(1)}, bf16[153,3584]{1,0:T(8,128)(2,1)S(1)}, u32[]{:S(2)}, u32[]{:S(2)}) collective-permute-start(bf16[153,3584]{1,0:T(8,128)(2,1)S(1)} %slice.86), channel_id=1, source_target_pairs={{0,3},{1,0},{2,1},{3,2},{4,7},{5,4},{6,5},{7,6},{8,11},{9,8},{10,9... | collective-permute-start | bytes 3290120 | tf_op jit(solution)/shard_map/ppermute | solution.py:28
  84.7 1.9 %collective-permute-start.6 = (bf16[144,3584]{1,0:T(8,128)(2,1)S(1)}, bf16[144,3584]{1,0:T(8,128)(2,1)}, u32[]{:S(2)}, u32[]{:S(2)}) collective-permute-start(bf16[144,3584]{1,0:T(8,128)(2,1)S(1)} %slice.85), channel_id=1, source_target_pairs={{0,1},{1,2},{2,3},{3,0},{4,5},{5,6},{6,7},{7,4},{8,9},{9,10},{10,1... | collective-permute-start | bytes 3096584 | tf_op jit(solution)/shard_map/ppermute | solution.py:28
  86.6 21.4 %collective-permute-done.7.refs_1_ = bf16[153,3584]{1,0:T(8,128)(2,1)S(1)} collective-permute-done((bf16[153,3584]{1,0:T(8,128)(2,1)S(1)}, bf16[153,3584]{1,0:T(8,128)(2,1)S(1)}, u32[]{:S(2)}, u32[]{:S(2)}) %collective-permute-start.7) | collective-permute-done | bytes 1096736 | tf_op jit(solution)/shard_map/ppermute | solution.py:28
  108.0 2.8 %collective-permute-start.9 = (bf16[153,3584]{1,0:T(8,128)(2,1)S(1)}, bf16[153,3584]{1,0:T(8,128)(2,1)}, u32[]{:S(2)}, u32[]{:S(2)}) collective-permute-start(bf16[153,3584]{1,0:T(8,128)(2,1)S(1)} %collective-permute-done.7.refs_1_), channel_id=1, source_target_pairs={{0,4},{4,0},{1,5},{5,1},{2,6},{6,2},{3,7},{7,3},{8,12},{12,8},{9,1... | collective-permute-start | bytes 3290120 | tf_op jit(solution)/shard_map/ppermute | solution.py:28
  112.0 3.0 %collective-permute-start.8 = (bf16[144,3584]{1,0:T(8,128)(2,1)}, bf16[144,3584]{1,0:T(8,128)(2,1)}, u32[]{:S(2)}, u32[]{:S(2)}) collective-permute-start(bf16[144,3584]{1,0:T(8,128)(2,1)} %collective-permute-done.6.refs_0_), channel_id=1, source_target_pairs={{0,4},{4,0},{1,5},{5,1},{2,6},{6,2},{3,7},{7,3},{8,12},{12,8},{9,1... | collective-permute-start | bytes 3096584 | tf_op jit(solution)/shard_map/ppermute | solution.py:28
  116.6 1.6 copy-done
  118.3 11.0 %shard_map.73 = (f32[8,256]{1,0:T(8,128)S(1)}, bf16[4,256,896]{2,1,0:T(8,128)(2,1)S(1)}, bf16[256,128]{1,0:T(8,128)(2,1)S(1)}) custom-call(s32[6]{0:T(128)S(1)} %stack.80.starts, bf16[1024,1024]{1,0:T(8,128)(2,1)S(1)} %bitcast.32, f32[8,256]{1,0:T(8,128)S(1)} %copy-done.1, bf16[297,3584]{1,0:T(8,128)(2,1)S(1)} %copy-done, ...), custom_call_target="tpu_custom_call" | custom-call | flops 3269984256 | bytes 12773376 | tf_op jit(solution)/shard_map/pallas_call | solution.py:132
  129.3 4.2 %shard_map.74.carried = f32[8,256]{1,0:T(8,128)S(1)} custom-call(s32[2]{0:T(128)S(1)} %pad_add_fusion.1.starts, bf16[4,256,896]{2,1,0:T(8,128)(2,1)S(1)} %get-tuple-element.20.tokens, bf16[256,128]{1,0:T(8,128)(2,1)S(1)} %get-tuple-element.21.notes, f32[8,256]{1,0:T(8,128)S(1)} %get-tuple-element.22.carried, ...), custom_call_target="tpu_custom_call" | custom-call | flops 544997376 | bytes 2128896 | tf_op jit(solution)/shard_map/pallas_call | solution.py:132
  133.5 4.2 %shard_map.75 = f32[8,256]{1,0:T(8,128)S(1)} custom-call(s32[2]{0:T(128)S(1)} %pad_add_fusion.starts, bf16[4,256,896]{2,1,0:T(8,128)(2,1)S(1)} %get-tuple-element.20.tokens, bf16[256,128]{1,0:T(8,128)(2,1)S(1)} %get-tuple-element.21.notes, f32[8,256]{1,0:T(8,128)S(1)} %shard_map.74.carried, bf16[144,3584]{1,0:T(8,128)(2,1)} %collective-permute-done.8.refs_0_, ...), custom_call_target="tpu_custom_call" | custom-call | flops 544997376 | bytes 2128896 | tf_op jit(solution)/shard_map/pallas_call | solution.py:132
  138.6 15.4 %all-to-all-start.2 = ((f32[64,1,16]{2,1,0:T(1,128)}), f32[64,1,16]{2,1,0:T(1,128)S(1)}, u32[]{:S(2)}, u32[]{:S(2)}) async-start(f32[64,1,16]{2,1,0:T(1,128)} %copy.32), calls=%async_computation.2 | async-start | bytes 65536 | tf_op jit(solution)/shard_map/all_to_all | solution.py:37
  154.3 10.6 %all-to-all-done.2 = f32[64,1,16]{2,1,0:T(1,128)S(1)} async-done(((f32[64,1,16]{2,1,0:T(1,128)}), f32[64,1,16]{2,1,0:T(1,128)S(1)}, u32[]{:S(2)}, u32[]{:S(2)}) %all-to-all-start.2) | async-done | bytes 4128 | tf_op jit(solution)/shard_map/all_to_all | solution.py:37
  165.1 6.5 %all_to_all.31 = f32[4,1,4]{2,1,0:T(1,128)S(1)} all-to-all(f32[4,1,4]{2,1,0:T(1,128)S(1)} %broadcast_in_dim.11), channel_id=1, replica_groups=mesh['dp_0'=8,'dp_1'=8,'dp_2'=2,'tensor'=4] {'tensor'}, dimensions={0} | all-to-all | bytes 128 | tf_op jit(solution)/shard_map/all_to_all | solution.py:37
  (63 shorter events, 11.7 us)
Async XLA Ops:
  1.6 9.6 %all-to-all-start = ((bf16[4,16,896]{2,1,0:T(8,128)(2,1)}), bf16[4,16,896]{2,1,0:T(8,128)(2,1)S(1)}, u32[]{:S(2)}, u32[]{:S(2)}) async-start(bf16[4,16,896]{2,1,0:T(8,128)(2,1)} %bitcast.3), calls=%async_computation | async-start | bytes 229376 | tf_op jit(solution)/shard_map/all_to_all | solution.py:37
  15.2 11.8 %collective-permute-start = (bf16[4,4,1024]{2,0,1:T(4,128)(2,1)S(1)}, bf16[4,4,1024]{2,0,1:T(4,128)(2,1)S(1)}, u32[]{:S(2)}, u32[]{:S(2)}) collective-permute-start(bf16[4,4,1024]{2,0,1:T(4,128)(2,1)S(1)} %fusion.6), channel_id=1, source_target_pairs={{0,4},{4,8},{8,12},{12,16},{16,20},{20,24},{24,28},{28,32},{32,36}... | collective-permute-start | bytes 98312 | tf_op jit(solution)/shard_map/ppermute | solution.py:33
  20.4 49.8 %collective-permute-start.1 = (bf16[297,3584]{1,0:T(8,128)(2,1)}, bf16[297,3584]{1,0:T(8,128)(2,1)}, u32[]{:S(2)}, u32[]{:S(2)}) collective-permute-start(bf16[297,3584]{1,0:T(8,128)(2,1)} %refs_0_), channel_id=1, source_target_pairs={{0,1},{1,2},{2,3},{3,0},{4,5},{5,6},{6,7},{7,4},{8,9},{9,10},{10,1... | collective-permute-start | bytes 6386696 | tf_op jit(solution)/shard_map/ppermute | solution.py:28
  22.6 52.9 %collective-permute-start.2 = (bf16[297,3584]{1,0:T(8,128)(2,1)}, bf16[297,3584]{1,0:T(8,128)(2,1)}, u32[]{:S(2)}, u32[]{:S(2)}) collective-permute-start(bf16[297,3584]{1,0:T(8,128)(2,1)} %refs_0_), channel_id=1, source_target_pairs={{0,3},{1,0},{2,1},{3,2},{4,7},{5,4},{6,5},{7,6},{8,11},{9,8},{10,9... | collective-permute-start | bytes 6386696 | tf_op jit(solution)/shard_map/ppermute | solution.py:28
  28.7 87.9 %all-to-all-start.1 = ((bf16[64,16,1024]{2,1,0:T(8,128)(2,1)}), bf16[64,16,1024]{2,1,0:T(8,128)(2,1)S(1)}, u32[]{:S(2)}, u32[]{:S(2)}) async-start(bf16[64,16,1024]{2,1,0:T(8,128)(2,1)} %broadcast_in_dim.10), calls=%async_computation.1 | async-start | bytes 4194304 | tf_op jit(solution)/shard_map/all_to_all | solution.py:37
  44.2 72.5 %copy-start.1 = (f32[8,256]{1,0:T(8,128)S(1)}, f32[8,256]{1,0:T(8,128)}, u32[]{:S(2)}) copy-start(f32[8,256]{1,0:T(8,128)} %constant.129.clone.1.carried) | copy-start | bytes 24580
  44.2 72.4 %collective-permute-start.3 = (bf16[297,3584]{1,0:T(8,128)(2,1)}, bf16[297,3584]{1,0:T(8,128)(2,1)}, u32[]{:S(2)}, u32[]{:S(2)}) collective-permute-start(bf16[297,3584]{1,0:T(8,128)(2,1)} %refs_0_), channel_id=1, source_target_pairs={{0,4},{4,0},{1,5},{5,1},{2,6},{6,2},{3,7},{7,3},{8,12},{12,8},{9,1... | collective-permute-start | bytes 6386696 | tf_op jit(solution)/shard_map/ppermute | solution.py:28
  70.3 46.4 %collective-permute-start.4 = (bf16[297,3584]{1,0:T(8,128)(2,1)}, bf16[297,3584]{1,0:T(8,128)(2,1)}, u32[]{:S(2)}, u32[]{:S(2)}) collective-permute-start(bf16[297,3584]{1,0:T(8,128)(2,1)} %collective-permute-done.1.refs_1_), channel_id=1, source_target_pairs={{0,4},{4,0},{1,5},{5,1},{2,6},{6,2},{3,7},{7,3},{8,12},{12,8},{9,1... | collective-permute-start | bytes 6386696 | tf_op jit(solution)/shard_map/ppermute | solution.py:28
  75.6 41.1 %collective-permute-start.5 = (bf16[297,3584]{1,0:T(8,128)(2,1)}, bf16[297,3584]{1,0:T(8,128)(2,1)}, u32[]{:S(2)}, u32[]{:S(2)}) collective-permute-start(bf16[297,3584]{1,0:T(8,128)(2,1)} %collective-permute-done.2.refs_2_), channel_id=1, source_target_pairs={{0,4},{4,0},{1,5},{5,1},{2,6},{6,2},{3,7},{7,3},{8,12},{12,8},{9,1... | collective-permute-start | bytes 6386696 | tf_op jit(solution)/shard_map/ppermute | solution.py:28
  78.8 29.2 %collective-permute-start.7 = (bf16[153,3584]{1,0:T(8,128)(2,1)S(1)}, bf16[153,3584]{1,0:T(8,128)(2,1)S(1)}, u32[]{:S(2)}, u32[]{:S(2)}) collective-permute-start(bf16[153,3584]{1,0:T(8,128)(2,1)S(1)} %slice.86), channel_id=1, source_target_pairs={{0,3},{1,0},{2,1},{3,2},{4,7},{5,4},{6,5},{7,6},{8,11},{9,8},{10,9... | collective-permute-start | bytes 3290120 | tf_op jit(solution)/shard_map/ppermute | solution.py:28
  84.7 27.3 %collective-permute-start.6 = (bf16[144,3584]{1,0:T(8,128)(2,1)S(1)}, bf16[144,3584]{1,0:T(8,128)(2,1)}, u32[]{:S(2)}, u32[]{:S(2)}) collective-permute-start(bf16[144,3584]{1,0:T(8,128)(2,1)S(1)} %slice.85), channel_id=1, source_target_pairs={{0,1},{1,2},{2,3},{3,0},{4,5},{5,6},{6,7},{7,4},{8,9},{9,10},{10,1... | collective-permute-start | bytes 3096584 | tf_op jit(solution)/shard_map/ppermute | solution.py:28
  108.0 25.5 %collective-permute-start.9 = (bf16[153,3584]{1,0:T(8,128)(2,1)S(1)}, bf16[153,3584]{1,0:T(8,128)(2,1)}, u32[]{:S(2)}, u32[]{:S(2)}) collective-permute-start(bf16[153,3584]{1,0:T(8,128)(2,1)S(1)} %collective-permute-done.7.refs_1_), channel_id=1, source_target_pairs={{0,4},{4,0},{1,5},{5,1},{2,6},{6,2},{3,7},{7,3},{8,12},{12,8},{9,1... | collective-permute-start | bytes 3290120 | tf_op jit(solution)/shard_map/ppermute | solution.py:28
  112.0 21.5 %collective-permute-start.8 = (bf16[144,3584]{1,0:T(8,128)(2,1)}, bf16[144,3584]{1,0:T(8,128)(2,1)}, u32[]{:S(2)}, u32[]{:S(2)}) collective-permute-start(bf16[144,3584]{1,0:T(8,128)(2,1)} %collective-permute-done.6.refs_0_), channel_id=1, source_target_pairs={{0,4},{4,0},{1,5},{5,1},{2,6},{6,2},{3,7},{7,3},{8,12},{12,8},{9,1... | collective-permute-start | bytes 3096584 | tf_op jit(solution)/shard_map/ppermute | solution.py:28
  116.6 1.6 copy-start
  133.5 20.6 %copy-start.2 = (s32[4]{0:T(128)S(1)}, s32[4]{0:T(128)}, u32[]{:S(2)}) copy-start(s32[4]{0:T(128)} %param.12) | copy-start | bytes 52
  138.6 26.3 %all-to-all-start.2 = ((f32[64,1,16]{2,1,0:T(1,128)}), f32[64,1,16]{2,1,0:T(1,128)S(1)}, u32[]{:S(2)}, u32[]{:S(2)}) async-start(f32[64,1,16]{2,1,0:T(1,128)} %copy.32), calls=%async_computation.2 | async-start | bytes 65536 | tf_op jit(solution)/shard_map/all_to_all | solution.py:37
